TPU v7x, 128 devices: a whole 4x4x4 slice. The times are simulated.
128 devices in a mesh: rows: 32 (over x, z, core), feat: 4 (over y).
Axes of the slice: x: 4, y: 4, z: 4, core: 2. Of those that a mesh axis runs over, the one named last changes fastest.
Arguments:
- bins: int32 [256, 49152], P('feat', 'rows'), may hold values from 0 to 255
- gradients: bfloat16 [49152], P('rows'), may hold values from -11 to 14
- hessians: bfloat16 [49152], P('rows'), may hold values from 0.099609375 to 1
- predictions: float32 [49152], P('rows'), may hold values from -6 to 6
- leaf: int32 [49152], P('rows'), may hold values from 0 to 7
- split_feature: int32 [8], replicated, may hold values from 0 to 255
- split_bin: int32 [8], replicated, may hold values from 0 to 254
- row_counts: int32 [32], P('rows'), may hold values from 96 to 1536, as said below
Outputs:
- hist: float32 [4, 64, 2, 16, 256], P('feat', 'rows')
- new_leaf: int32 [49152], P('rows')
- new_pred: float32 [49152], P('rows')
Inputs may be any that keep to these rules, and one draw needn't show every extreme that they name: `row_counts`: some sweep batch has all 1536 rows live.
All inputs are finite; a program needn't handle non-finite values.
Results may differ from a plain program's by a relative error of at most 0.0003.
Values may be sent and summed in bfloat16 or wider, within the bound.
No kernel may reach another device: no remote copies, remote signals or barrier semaphores. Data moves between devices by JAX's collectives and lax.ppermute only.
A program may use at most 128 MiB of HBM per device.

v0:
```python
import math

import jax
import jax.numpy as jnp
from jax import lax
from jax.sharding import PartitionSpec as P

B = 256
LEAVES = 8


def joined_along(parts, dim):
    dims = list(parts.shape[1:])
    dims[dim] *= parts.shape[0]
    return jnp.moveaxis(parts, 0, dim).reshape(dims)


def from_everyone(value, axis):
    copies = jnp.broadcast_to(value, (lax.axis_size(axis), *value.shape))
    return lax.all_to_all(copies, axis, split_axis=0, concat_axis=0, tiled=True)


def gathered_copies(value, axis, dim):
    return joined_along(from_everyone(value, axis), dim)


def in_blocks(value, dim, devices):
    before, after = (value.shape[:dim], value.shape[dim + 1 :])
    return jnp.moveaxis(value.reshape(*before, devices, -1, *after), dim, 0)


def sent_and_summed(value, axis, dim):
    devices = lax.axis_size(axis)
    parts = lax.all_to_all(in_blocks(value, dim, devices), axis, 0, 0, tiled=True)
    return jnp.sum(parts, axis=0)


def build_terms(columns, weights, blocks, blocking):
    width = columns.shape[0]
    kinds = weights.shape[0]
    levels = jnp.arange(B, dtype=jnp.int32)
    flipped = columns.T

    def add_block(step, accum):
        start = step * blocking
        cells = lax.dynamic_slice_in_dim(flipped, start, blocking, 0)
        wrows = lax.dynamic_slice_in_dim(weights, start, blocking, 1)
        table = (cells[:, :, None] == levels[None, None, :]).astype(jnp.bfloat16)
        table = table.reshape(blocking, width * B)
        return accum + jnp.dot(wrows, table, preferred_element_type=jnp.float32)

    accum = lax.fori_loop(0, blocks, add_block, jnp.zeros((kinds, width * B), jnp.float32))
    return accum.reshape(2, kinds // 2, width, B).transpose(2, 0, 1, 3)


def make_weights(member, grad_live, hess_live):
    zero = jnp.zeros((), jnp.bfloat16)
    upper = jnp.where(member, grad_live[None, :], zero)
    lower = jnp.where(member, hess_live[None, :], zero)
    return jnp.concatenate([upper, lower], 0)


def body(bins, gradients, hessians, predictions, leaf, split_feature, split_bin, row_counts):
    width, rows_here = bins.shape
    kids = 2 * LEAVES
    offset = lax.axis_index("feat") * width
    slots = jnp.arange(LEAVES, dtype=jnp.int32)
    match = leaf[:, None] == slots[None, :]
    wanted = jnp.sum(jnp.where(match, split_feature[None, :], 0), 1)
    cutoff = jnp.sum(jnp.where(match, split_bin[None, :], 0), 1)
    local = wanted - offset
    owned = (local >= 0) & (local < width)
    feature_ids = jnp.arange(width, dtype=jnp.int32)
    picked = feature_ids[:, None] == local[None, :]
    chosen = jnp.sum(jnp.where(picked, bins, 0), 0)
    flags = jnp.where(owned & (chosen > cutoff), 1.0, 0.0).astype(jnp.bfloat16)
    every = gathered_copies(flags, "feat", 0).reshape(-1, rows_here)
    merged = jnp.sum(every.astype(jnp.float32), 0)
    going = jnp.where(merged > 0.5, 1, 0).astype(jnp.int32)
    new_leaf = 2 * leaf + going
    live = jnp.arange(rows_here, dtype=jnp.int32) < row_counts[0]
    zero = jnp.zeros((), jnp.bfloat16)
    grad_live = jnp.where(live, gradients, zero)
    hess_live = jnp.where(live, hessians, zero)
    kid_slots = jnp.arange(kids, dtype=jnp.int32)
    member = new_leaf[None, :] == kid_slots[:, None]
    weights = make_weights(member, grad_live, hess_live)
    blocking = math.gcd(rows_here, 512)
    blocks = rows_here // blocking
    hist = sent_and_summed(build_terms(bins, weights, blocks, blocking), "rows", 0)
    totals = jnp.sum(hist[0], 2)
    value = -totals[0] / (totals[1] + 1.0)
    gained = jnp.sum(jnp.where(member, value[:, None], jnp.float32(0.0)), 0)
    new_pred = predictions + 0.5 * gained
    return (hist[None], new_leaf, new_pred)


def solution(mesh):
    in_specs = (P("feat", "rows"), P("rows"), P("rows"), P("rows"), P("rows"), P(), P(), P("rows"))
    out_specs = (P("feat", "rows", None, None, None), P("rows"), P("rows"))
    return jax.shard_map(body, mesh=mesh, in_specs=in_specs, out_specs=out_specs, check_vma=False)
```

profile of v0, /device:TPU:1, one launch (start us, length us, event | category | flops | bytes accessed | tf_op | source)
XLA Modules:
  0.0 198.8 jit_solution(5740868178283056570)
XLA Ops:
  0.6 0.8 select_reduce_fusion.2
  1.4 1.1 select_reduce_fusion
  2.6 0.5 broadcast.47
  3.1 0.7 reduce.2
  3.8 0.6 reshape.54
  4.4 5.0 %all-to-all-start = ((bf16[4,2,768]{2,1,0:T(2,128)(2,1)}), bf16[4,2,768]{2,1,0:T(2,128)(2,1)S(1)}, u32[]{:S(2)}, u32[]{:S(2)}) async-start(bf16[4,2,768]{2,1,0:T(2,128)(2,1)} %reshape.54), calls=%async_computation | async-start | bytes 24576 | tf_op jit(solution)/shard_map/all_to_all | solution.py:20
  10.0 0.7 fusion.12
  10.8 1.3 copy.36
  12.0 1.6 all-to-all-done
  13.6 0.7 select_add_fusion
  14.3 0.0 copy-start
  14.4 0.6 copy-done
  14.9 137.9 %while.14 = (s32[]{:T(128)}, f32[32,16384]{1,0:T(8,128)}, bf16[32,1536]{1,0:T(8,128)(2,1)S(1)}, s32[1536,64]{1,0:T(8,128)S(1)}, s32[]{:T(128)}, /*index=5*/s32[]{:T(128)}, s32[]{:T(128)}, s32[]{:T(128)}) while((s32[]{:T(128)}, f32[32,16384]{1,0:T(8,128)}, bf16[32,1536]{1,0:T(8,128)(2,1)S(1)}, s32[1536,64]{1,0:T(8,128)S(1)}, ...), condition=%wide.region_5.6_spmd.clone, body=%wide.region_4.5_spmd.clone.sunk | while | flops 546308096 | bytes 139100320 | solution.py:52
  15.0 4.9 %eq.139 = s32[512,64,256]{2,1,0:T(8,128)S(1)} broadcast(s32[512,64]{1,0:T(8,128)S(1)} %constant_dynamic-slice_fusion.2), dimensions={0,1} | broadcast | bytes 33685504 | tf_op jit(solution)/shard_map/while/body/eval_jaxpr/eq | solution.py:48
  19.9 25.6 %copy.48 = s32[64,8,64,256]{3,1,2,0:T(8,128)} copy(s32[64,8,64,256]{3,2,1,0:T(8,128)S(1)} %bitcast.28) | data formatting | bytes 67108864 | tf_op jit(solution)/shard_map/while
  45.5 15.0 %fusion.20 = f32[32,16384]{1,0:T(8,128)} fusion(s32[512,16384]{1,0:T(8,128)} %bitcast.27, s32[16384]{0:T(1024)S(1)} %bitcast.32, f32[32,16384]{1,0:T(8,128)} %get-tuple-element.181, pred[]{:T(512)S(6)} %compare.3, bf16[32,1536]{1,0:T(8,128)(2,1)S(1)} %get-tuple-element.190, s32[]{:T(128)S(6)} %select_n.67), kind=kOutput, calls=%fused_computation.3.clone.1 | convolution fusion | flops 546308096 | bytes 37847044 | tf_op jit(solution)/shard_map/while/body/eval_jaxpr/dot_general | solution.py:50
  60.5 4.9 %eq.139 = s32[512,64,256]{2,1,0:T(8,128)S(1)} broadcast(s32[512,64]{1,0:T(8,128)S(1)} %constant_dynamic-slice_fusion.2), dimensions={0,1} | broadcast | bytes 33685504 | tf_op jit(solution)/shard_map/while/body/eval_jaxpr/eq | solution.py:48
  65.4 25.6 %copy.48 = s32[64,8,64,256]{3,1,2,0:T(8,128)} copy(s32[64,8,64,256]{3,2,1,0:T(8,128)S(1)} %bitcast.28) | data formatting | bytes 67108864 | tf_op jit(solution)/shard_map/while
  91.0 15.6 %fusion.20 = f32[32,16384]{1,0:T(8,128)} fusion(s32[512,16384]{1,0:T(8,128)} %bitcast.27, s32[16384]{0:T(1024)S(1)} %bitcast.32, f32[32,16384]{1,0:T(8,128)} %get-tuple-element.181, pred[]{:T(512)S(6)} %compare.3, bf16[32,1536]{1,0:T(8,128)(2,1)S(1)} %get-tuple-element.190, s32[]{:T(128)S(6)} %select_n.67), kind=kOutput, calls=%fused_computation.3.clone.1 | convolution fusion | flops 546308096 | bytes 37847044 | tf_op jit(solution)/shard_map/while/body/eval_jaxpr/dot_general | solution.py:50
  106.7 4.9 %eq.139 = s32[512,64,256]{2,1,0:T(8,128)S(1)} broadcast(s32[512,64]{1,0:T(8,128)S(1)} %constant_dynamic-slice_fusion.2), dimensions={0,1} | broadcast | bytes 33685504 | tf_op jit(solution)/shard_map/while/body/eval_jaxpr/eq | solution.py:48
  111.6 25.6 %copy.48 = s32[64,8,64,256]{3,1,2,0:T(8,128)} copy(s32[64,8,64,256]{3,2,1,0:T(8,128)S(1)} %bitcast.28) | data formatting | bytes 67108864 | tf_op jit(solution)/shard_map/while
  137.2 15.6 %fusion.20 = f32[32,16384]{1,0:T(8,128)} fusion(s32[512,16384]{1,0:T(8,128)} %bitcast.27, s32[16384]{0:T(1024)S(1)} %bitcast.32, f32[32,16384]{1,0:T(8,128)} %get-tuple-element.181, pred[]{:T(512)S(6)} %compare.3, bf16[32,1536]{1,0:T(8,128)(2,1)S(1)} %get-tuple-element.190, s32[]{:T(128)S(6)} %select_n.67), kind=kOutput, calls=%fused_computation.3.clone.1 | convolution fusion | flops 546308096 | bytes 37847044 | tf_op jit(solution)/shard_map/while/body/eval_jaxpr/dot_general | solution.py:50
  152.8 2.2 %copy.44 = f32[4,8,64,256]{3,2,1,0:T(8,128)S(1)} copy(f32[4,8,64,256]{3,1,2,0:T(8,128)} %bitcast.29) | data formatting | bytes 4194304
  155.0 0.2 bitcast_bitcast_fusion
  155.3 1.2 copy.37
  156.5 2.0 copy.38
  158.4 38.0 %all_to_all.11 = f32[32,2,2,16,256]{4,1,3,2,0:T(2,128)S(1)} all-to-all(f32[32,2,2,16,256]{4,1,3,2,0:T(2,128)S(1)} %copy.38), channel_id=1, replica_groups=mesh['rows'=32,'feat'=4] {'rows'}, dimensions={0} | all-to-all | bytes 4194304 | tf_op jit(solution)/shard_map/all_to_all | solution.py:34
  196.4 0.0 copy-start.1
  196.4 0.0 copy-start.2
  196.4 0.8 reduce_sum.67
  197.3 0.2 slice_reduce_fusion
  197.5 0.0 copy-done.1
  197.5 0.1 select_reduce_fusion.1
  197.6 0.6 copy.40
  198.2 0.0 copy-done.2
  198.2 0.6 multiply_add_fusion
  (18 shorter events, 0.3 us)
Async XLA Ops:
  4.4 9.2 %all-to-all-start = ((bf16[4,2,768]{2,1,0:T(2,128)(2,1)}), bf16[4,2,768]{2,1,0:T(2,128)(2,1)S(1)}, u32[]{:S(2)}, u32[]{:S(2)}) async-start(bf16[4,2,768]{2,1,0:T(2,128)(2,1)} %reshape.54), calls=%async_computation | async-start | bytes 24576 | tf_op jit(solution)/shard_map/all_to_all | solution.py:20
  14.3 0.6 copy-start
  196.4 1.1 copy-start.1
  196.4 1.8 copy-start.2
where the time goes:
time: 199 us
  local copies, waits for them, and re-layouts  101 us (51%)
  matrix products  46.3 us (23%)
  blocking collectives  38 us (19%)
  other arithmetic  5.81 us (3%)
  starting transfers between devices  5 us (3%)
    while x9, local copies, waits for them, and re-layouts  76.8 us
    dot_general x3, matrix products, add_block(): return accum + jnp.dot(wrows, table, preferred_element_type=jnp.float32)  46.3 us
    all_to_all x1, blocking collectives, sent_and_summed(): lax.all_to_all(in_blocks(value, dim, devices), axis, 0, 0, tiled=True)  38 us
    eq x3, local copies, waits for them, and re-layouts, add_block(): table = (cells[:, :, None] == levels[None, None, :]).astype(jnp.bfloat16)  14.7 us
    unnamed x11, local copies, waits for them, and re-layouts  5.32 us
    all_to_all x1, starting transfers between devices, from_everyone(): return lax.all_to_all(copies, axis, split_axis=0, concat_axis=0, tiled=True)  5 us
  transfers between devices with their start and end apart: 1, of which 1 were waited for; matrix products, arithmetic and copies ran while one was open for 1% of the time, Pallas kernels for 0%

commit v1 on v0

v1 whole, which is shorter than its diff:
```python
import jax
import jax.numpy as jnp
from jax import lax
from jax.experimental import pallas as pl
from jax.experimental.pallas import tpu as pltpu
from jax.sharding import PartitionSpec as P

B = 256
LEAVES = 8
KIDS = 2 * LEAVES
LANES = 128
GROUP = 16
VMEM = pl.BlockSpec(memory_space=pltpu.VMEM)
SMALL = pltpu.CompilerParams(vmem_limit_bytes=16 << 20)
SMEM = pl.BlockSpec(memory_space=pltpu.SMEM)


def split_kernel(features, cutoffs, bins, leaf, part, packed, rows):
    width, length = bins.shape
    blocks = length // LANES
    for top in range(0, width, 8):
        for k in range(blocks):
            rows[pl.ds(top * blocks + k, 8, stride=blocks), :] = bins[top : top + 8, k * LANES : (k + 1) * LANES]
    first = lax.axis_index("feat") * width
    leaves = leaf[...]
    code = jnp.zeros((blocks, LANES), jnp.int32)
    for slot in range(LEAVES):
        local = features[slot] - first
        here = ((local >= 0) & (local < width)).astype(jnp.int32)
        chosen = rows[pl.ds(jnp.clip(local, 0, width - 1) * blocks, blocks), :]
        child = (2 * slot + (chosen > cutoffs[slot]).astype(jnp.int32)) * here
        code = jnp.where(leaves == slot, child, code)
    part[...] = code.astype(jnp.float32).astype(jnp.bfloat16)
    owners, each, _ = packed.shape
    for owner in range(owners):
        packed[owner] = rows[owner * each : (owner + 1) * each, :].astype(jnp.float32).astype(jnp.bfloat16)


def fill_kernel(count, packed, gradients, hessians, mine, one, two, three, send, new_leaf, stage):
    owners, each, _ = packed.shape
    blocks = mine.shape[0]
    code = sum(x[...].astype(jnp.float32) for x in (mine, one, two, three))
    new_leaf[...] = code.astype(jnp.int32)
    spot = lax.broadcasted_iota(jnp.int32, (blocks, LANES), 0) * LANES
    spot = spot + lax.broadcasted_iota(jnp.int32, (blocks, LANES), 1)
    live = spot < count[0]
    stage[0:blocks, :] = jnp.where(live, gradients[...].astype(jnp.float32), 0.0)
    stage[blocks : 2 * blocks, :] = jnp.where(live, hessians[...].astype(jnp.float32), 0.0)
    stage[2 * blocks : 3 * blocks, :] = code
    used = (count[0] + LANES - 1) // LANES
    rest = stage.shape[0] - 3 * blocks
    stage[3 * blocks :, :] = jnp.full((rest, LANES), used, jnp.int32).astype(jnp.float32)
    tail = stage[...].astype(jnp.bfloat16)
    for owner in range(owners):
        send[owner, 0:each, :] = packed[owner]
        send[owner, each:, :] = tail


def hist_kernel(recv, new_leaf, predictions, hist, new_pred, wide, columns, accum):
    sources, height, _ = recv.shape
    blocks = new_leaf.shape[0]
    each = recv.shape[1]
    for s in range(sources):
        wide[s * each : (s + 1) * each, :] = recv[s].astype(jnp.float32)
    place = 0
    for s in range(sources):
        for j in range(5):
            columns[j, pl.ds(place, blocks), :] = wide[s * each + j * blocks : s * each + (j + 1) * blocks, :]
        used = wide[s * each + 5 * blocks : s * each + 5 * blocks + 1, :][0, 0].astype(jnp.int32)
        place = place + used
    for j in range(5):
        columns[j, pl.ds(place, GROUP), :] = jnp.zeros((GROUP, LANES), jnp.float32)
    accum[...] = jnp.zeros(accum.shape, jnp.float32)
    slots = lax.broadcasted_iota(jnp.int32, (2 * KIDS, LANES), 0).astype(jnp.float32).astype(jnp.bfloat16)
    levels = lax.broadcasted_iota(jnp.int32, (LANES, LANES), 0).astype(jnp.float32).astype(jnp.bfloat16)
    zero = jnp.zeros((), jnp.bfloat16)
    one = jnp.ones((), jnp.bfloat16)

    def spread(row, height):
        return jnp.broadcast_to(row, (height, LANES)).astype(jnp.bfloat16)

    def step(i, carry):
        base = i * GROUP
        uppers = [[], []]
        lowers = [[], []]
        for k in range(GROUP):
            at = base + k
            grad = spread(columns[2, pl.ds(at, 1), :], 2 * KIDS)
            hess = spread(columns[3, pl.ds(at, 1), :], 2 * KIDS)
            child = columns[4, pl.ds(at, 1), :]
            for f in range(2):
                cell = columns[f, pl.ds(at, 1), :]
                high = cell >= LANES
                low = spread(jnp.where(high, cell - LANES, cell), LANES)
                slot = spread(jnp.where(high, child + KIDS, child), 2 * KIDS)
                hit = slot == slots
                uppers[f].append(jnp.concatenate([jnp.where(hit, grad, zero), jnp.where(hit, hess, zero)], 0))
                lowers[f].append(jnp.where(low == levels, one, zero))
        for f in range(2):
            upper = jnp.concatenate(uppers[f], 1)
            lower = jnp.concatenate(lowers[f], 1)
            accum[f] += lax.dot_general(upper, lower, (((1,), (1,)), ((), ())), preferred_element_type=jnp.float32)
        return carry

    lax.fori_loop(0, (place + GROUP - 1) // GROUP, step, 0)
    for f in range(2):
        for kind in range(2):
            for high in range(2):
                top = (kind * 2 + high) * KIDS
                hist[f, kind, :, high * LANES : (high + 1) * LANES] = accum[f, top : top + KIDS, :]
    sums = [jnp.sum(accum[0, top : top + KIDS, :] + accum[0, top + KIDS : top + 2 * KIDS, :], 1, keepdims=True) for top in (0, 2 * KIDS)]
    value = -sums[0] / (sums[1] + 1.0)
    kids = new_leaf[...]
    gained = jnp.zeros(kids.shape, jnp.float32)
    for c in range(KIDS):
        gained = jnp.where(kids == c, jnp.broadcast_to(value[c : c + 1, :], kids.shape), gained)
    new_pred[...] = predictions[...] + 0.5 * gained


def body(bins, gradients, hessians, predictions, leaf, split_feature, split_bin, row_counts):
    width, length = bins.shape
    blocks = length // LANES
    owners = lax.axis_size("rows")
    feats = lax.axis_size("feat")
    each = width // owners * blocks
    shape = jax.ShapeDtypeStruct
    tall = lambda x: x.reshape(blocks, LANES)
    part, packed = pl.pallas_call(
        split_kernel,
        out_shape=(shape((blocks, LANES), jnp.bfloat16), shape((owners, each, LANES), jnp.bfloat16)),
        in_specs=[SMEM, SMEM, VMEM, VMEM],
        out_specs=(VMEM, VMEM),
        scratch_shapes=[pltpu.VMEM((width * blocks, LANES), jnp.int32)],
        name="split_rows",
        compiler_params=SMALL,
    )(split_feature, split_bin, bins, tall(leaf))
    others = [lax.ppermute(part, "feat", [(i, (i + s) % feats) for i in range(feats)]) for s in range(1, feats)]
    height = each + 3 * blocks + 4
    send, new_leaf = pl.pallas_call(
        fill_kernel,
        out_shape=(shape((owners, height, LANES), jnp.bfloat16), shape((blocks, LANES), jnp.int32)),
        in_specs=[SMEM] + [VMEM] * 7,
        out_specs=(VMEM, VMEM),
        scratch_shapes=[pltpu.VMEM((height - each, LANES), jnp.float32)],
        name="fill_messages",
        compiler_params=SMALL,
    )(row_counts, packed, tall(gradients), tall(hessians), part, *others)
    recv = lax.all_to_all(send, "rows", 0, 0, tiled=True)
    hist, new_pred = pl.pallas_call(
        hist_kernel,
        out_shape=(shape((2, 2, KIDS, B), jnp.float32), shape((blocks, LANES), jnp.float32)),
        in_specs=[VMEM] * 3,
        out_specs=(VMEM, VMEM),
        scratch_shapes=[
            pltpu.VMEM((owners * height, LANES), jnp.float32),
            pltpu.VMEM((5, owners * blocks + GROUP, LANES), jnp.float32),
            pltpu.VMEM((2, 4 * KIDS, LANES), jnp.float32),
        ],
        name="histograms",
        compiler_params=SMALL,
    )(recv, new_leaf, tall(predictions))
    return (hist[None], new_leaf.reshape(-1), new_pred.reshape(-1))


def solution(mesh):
    in_specs = (P("feat", "rows"), P("rows"), P("rows"), P("rows"), P("rows"), P(), P(), P("rows"))
    out_specs = (P("feat", "rows", None, None, None), P("rows"), P("rows"))
    return jax.shard_map(body, mesh=mesh, in_specs=in_specs, out_specs=out_specs, check_vma=False)
```

time: 199 us -> 40.4 us (0.20)
  local copies, waits for them, and re-layouts: 101 us -> 2.37 us
  matrix products: 46.3 us -> 0 us
  blocking collectives: 38 us -> 21.8 us
  Pallas kernels: 0 us -> 7.09 us
  other arithmetic: 5.81 us -> 0 us
    while x9 -> x0, local copies, waits for them, and re-layouts: 76.8 us -> none
    dot_general x3 -> x0, matrix products: 46.3 us -> none  [add_block(): return accum + jnp.dot(wrows, table, preferred_element_type=jnp.float32)]
    all_to_all x1, blocking collectives: 38 us -> 21.8 us  [body(): recv = lax.all_to_all(send, 'rows', 0, 0, tiled=True)]
    eq x3 -> x0, local copies, waits for them, and re-layouts: 14.7 us -> none  [add_block(): table = (cells[:, :, None] == levels[None, None, :]).astype(jnp.bfloat16)]
    pallas_call x0 -> x3, Pallas kernels: none -> 7.09 us  [the longest x1 5.82 us: body(): pl.pallas_call(hist_kernel, out_shape=(shape((2, 2, KIDS, B), jnp.float32...]
    all_to_all x1 -> x0, starting transfers between devices: 5 us -> none  [from_everyone(): return lax.all_to_all(copies, axis, split_axis=0, concat_axis=0, tiled=True)]
    ppermute x0 -> x3, starting transfers between devices: none -> 4.66 us  [body(): lax.ppermute(part, 'feat', [(i, (i + s) % feats) for i in range(feats)])]
    reduce_sum x6 -> x0, other arithmetic: 3.02 us -> none  [the longest x1 1.06 us: body(): chosen = jnp.sum(jnp.where(picked, bins, 0), 0)]
  transfers between devices with their start and end apart: 1 -> 3, of which waited for: 1 -> 2; matrix products, arithmetic and copies ran while one was open for 1% -> 0% of each run, Pallas kernels for 0% -> 0%
where the time goes in v1:
time: 40.4 us; the launch traced here: 39.6 us
  blocking collectives  21.8 us (54%)
  Pallas kernels  7.09 us (18%)
  starting transfers between devices  4.66 us (12%)
  local copies, waits for them, and re-layouts  2.37 us (6%)
  waiting for transfers between devices  2.32 us (6%)
  between operations  1.34 us (3%)
    all_to_all x1, blocking collectives, body(): recv = lax.all_to_all(send, 'rows', 0, 0, tiled=True)  21.8 us
    pallas_call x1, Pallas kernels, body(): pl.pallas_call(hist_kernel, out_shape=(shape((2, 2, KIDS, B), jnp.float32...  5.82 us
    ppermute x3, starting transfers between devices, body(): lax.ppermute(part, 'feat', [(i, (i + s) % feats) for i in range(feats)])  4.66 us
    unnamed x16, local copies, waits for them, and re-layouts  2.37 us
    ppermute x3, waiting for transfers between devices, body(): lax.ppermute(part, 'feat', [(i, (i + s) % feats) for i in range(feats)])  2.32 us
  transfers between devices with their start and end apart: 3, of which 2 were waited for; matrix products, arithmetic and copies ran while one was open for 0% of the time, Pallas kernels for 0%

profile of v1, /device:TPU:1, one launch (start us, length us, event | category | flops | bytes accessed | tf_op | source)
XLA Modules:
  0.0 39.6 jit_solution(15092816512279682129)
XLA Ops:
  0.6 0.0 copy-start.7
  0.6 0.0 copy-start.6
  0.7 0.6 %copy-done.7 = s32[8]{0:T(128)S(1)} copy-done((s32[8]{0:T(128)S(1)}, s32[8]{0:T(128)}, u32[]{:S(2)}) %copy-start.7) | copy-done | bytes 56
  1.3 0.0 copy-done.6
  1.3 0.0 copy-start
  1.3 1.0 %copy-done = s32[64,1536]{1,0:T(8,128)S(1)} copy-done((s32[64,1536]{1,0:T(8,128)S(1)}, s32[64,1536]{1,0:T(8,128)}, u32[]{:S(2)}) %copy-start) | copy-done | bytes 393240
  2.3 0.0 copy-start.3
  2.3 0.7 %copy-done.3 = s32[1536]{0:T(1024)S(1)} copy-done((s32[1536]{0:T(1024)S(1)}, s32[1536]{0:T(1024)}, u32[]{:S(2)}) %copy-start.3) | copy-done | bytes 6168
  3.0 0.6 %split_rows.1 = (bf16[12,128]{1,0:T(8,128)(2,1)S(1)}, bf16[32,24,128]{2,1,0:T(8,128)(2,1)S(1)}) custom-call(s32[8]{0:T(128)S(1)} %copy-done.6, s32[8]{0:T(128)S(1)} %copy-done.7, s32[64,1536]{1,0:T(8,128)S(1)} %copy-done, s32[12,128]{1,0:T(8,128)S(1)} %bitcast.9), custom_call_target="tpu_custom_call" | custom-call | tf_op jit(solution)/shard_map/split_rows/pallas_call | solution.py:128
  3.6 0.0 copy-start.5
  3.6 0.0 copy-start.4
  3.6 3.6 %collective-permute-start.2 = (bf16[12,128]{1,0:T(8,128)(2,1)S(1)}, bf16[12,128]{1,0:T(8,128)(2,1)S(1)}, u32[]{:S(2)}, u32[]{:S(2)}) collective-permute-start(bf16[12,128]{1,0:T(8,128)(2,1)S(1)} %get-tuple-element.10.mine), channel_id=1, source_target_pairs={{0,3},{1,0},{2,1},{3,2},{4,7},{5,4},{6,5},{7,6},{8,11},{9,8},{10,9... | collective-permute-start | bytes 9224 | tf_op jit(solution)/shard_map/ppermute | solution.py:137
  7.3 0.3 collective-permute-start.1
  7.6 0.7 %collective-permute-start = (bf16[12,128]{1,0:T(8,128)(2,1)S(1)}, bf16[12,128]{1,0:T(8,128)(2,1)S(1)}, u32[]{:S(2)}, u32[]{:S(2)}) collective-permute-start(bf16[12,128]{1,0:T(8,128)(2,1)S(1)} %get-tuple-element.10.mine), channel_id=1, source_target_pairs={{0,1},{1,2},{2,3},{3,0},{4,5},{5,6},{6,7},{7,4},{8,9},{9,10},{10,1... | collective-permute-start | bytes 9224 | tf_op jit(solution)/shard_map/ppermute | solution.py:137
  9.0 0.0 collective-permute-done.2.three
  9.0 2.3 %collective-permute-done.1.two = bf16[12,128]{1,0:T(8,128)(2,1)S(1)} collective-permute-done((bf16[12,128]{1,0:T(8,128)(2,1)S(1)}, bf16[12,128]{1,0:T(8,128)(2,1)S(1)}, u32[]{:S(2)}, u32[]{:S(2)}) %collective-permute-start.1) | collective-permute-done | bytes 3104 | tf_op jit(solution)/shard_map/ppermute | solution.py:137
  11.2 0.1 collective-permute-done.one
  11.3 0.0 copy-done.5
  11.3 0.0 copy-done.4
  11.3 0.7 %fill_messages.1 = (bf16[32,64,128]{2,1,0:T(8,128)(2,1)S(1)}, s32[12,128]{1,0:T(8,128)}) custom-call(s32[1]{0:T(128)S(6)} %copy.11.count, bf16[32,24,128]{2,1,0:T(8,128)(2,1)S(1)} %get-tuple-element.9.packed, bf16[12,128]{1,0:T(8,128)(2,1)S(1)} %bitcast.10, bf16[12,128]{1,0:T(8,128)(2,1)S(1)} %bitcast.11, bf16[12,128]{1,0:T(8,128)(2,1)S(1)} %get-tuple-element.10.mine, ...), custom_call_target="tpu_custom_call" | custom-call | tf_op jit(solution)/shard_map/fill_messages/pallas_call | solution.py:139
  11.9 0.0 copy-start.1
  11.9 0.0 copy-start.2
  11.9 21.8 %all_to_all.5.recv = bf16[32,64,128]{2,1,0:T(8,128)(2,1)S(1)} all-to-all(bf16[32,64,128]{2,1,0:T(8,128)(2,1)S(1)} %get-tuple-element.11), channel_id=1, replica_groups=mesh['rows'=32,'feat'=4] {'rows'}, dimensions={0} | all-to-all | bytes 1048576 | tf_op jit(solution)/shard_map/all_to_all | solution.py:148
  33.8 0.0 copy-done.1
  33.8 0.0 copy-done.2
  33.8 5.8 %histograms.1 = (f32[2,2,16,256]{3,2,1,0:T(8,128)}, f32[12,128]{1,0:T(8,128)}) custom-call(bf16[32,64,128]{2,1,0:T(8,128)(2,1)S(1)} %all_to_all.5.recv, s32[12,128]{1,0:T(8,128)S(1)} %copy-done.2, f32[12,128]{1,0:T(8,128)S(1)} %bitcast.7), custom_call_target="tpu_custom_call" | custom-call | tf_op jit(solution)/shard_map/histograms/pallas_call | solution.py:149
Async XLA Ops:
  0.6 0.7 %copy-start.7 = (s32[8]{0:T(128)S(1)}, s32[8]{0:T(128)}, u32[]{:S(2)}) copy-start(s32[8]{0:T(128)} %cutoffs.1) | copy-start | bytes 100
  0.6 0.7 %copy-start.6 = (s32[8]{0:T(128)S(1)}, s32[8]{0:T(128)}, u32[]{:S(2)}) copy-start(s32[8]{0:T(128)} %features.1) | copy-start | bytes 100
  1.3 1.0 %copy-start = (s32[64,1536]{1,0:T(8,128)S(1)}, s32[64,1536]{1,0:T(8,128)}, u32[]{:S(2)}) copy-start(s32[64,1536]{1,0:T(8,128)} %bins.1) | copy-start | bytes 1179652
  2.3 0.7 %copy-start.3 = (s32[1536]{0:T(1024)S(1)}, s32[1536]{0:T(1024)}, u32[]{:S(2)}) copy-start(s32[1536]{0:T(1024)} %param.12) | copy-start | bytes 18436
  3.6 7.7 %copy-start.5 = (bf16[1536]{0:T(1024)(128)(2,1)S(1)}, bf16[1536]{0:T(1024)(128)(2,1)}, u32[]{:S(2)}) copy-start(bf16[1536]{0:T(1024)(128)(2,1)} %param.10) | copy-start | bytes 9220
  3.6 7.7 %copy-start.4 = (bf16[1536]{0:T(1024)(128)(2,1)S(1)}, bf16[1536]{0:T(1024)(128)(2,1)}, u32[]{:S(2)}) copy-start(bf16[1536]{0:T(1024)(128)(2,1)} %param.9) | copy-start | bytes 9220
  3.6 5.3 %collective-permute-start.2 = (bf16[12,128]{1,0:T(8,128)(2,1)S(1)}, bf16[12,128]{1,0:T(8,128)(2,1)S(1)}, u32[]{:S(2)}, u32[]{:S(2)}) collective-permute-start(bf16[12,128]{1,0:T(8,128)(2,1)S(1)} %get-tuple-element.10.mine), channel_id=1, source_target_pairs={{0,3},{1,0},{2,1},{3,2},{4,7},{5,4},{6,5},{7,6},{8,11},{9,8},{10,9... | collective-permute-start | bytes 9224 | tf_op jit(solution)/shard_map/ppermute | solution.py:137
  7.3 4.0 %collective-permute-start.1 = (bf16[12,128]{1,0:T(8,128)(2,1)S(1)}, bf16[12,128]{1,0:T(8,128)(2,1)S(1)}, u32[]{:S(2)}, u32[]{:S(2)}) collective-permute-start(bf16[12,128]{1,0:T(8,128)(2,1)S(1)} %get-tuple-element.10.mine), channel_id=1, source_target_pairs={{0,2},{1,3},{2,0},{3,1},{4,6},{5,7},{6,4},{7,5},{8,10},{9,11},{10,... | collective-permute-start | bytes 9224 | tf_op jit(solution)/shard_map/ppermute | solution.py:137
  7.6 3.7 %collective-permute-start = (bf16[12,128]{1,0:T(8,128)(2,1)S(1)}, bf16[12,128]{1,0:T(8,128)(2,1)S(1)}, u32[]{:S(2)}, u32[]{:S(2)}) collective-permute-start(bf16[12,128]{1,0:T(8,128)(2,1)S(1)} %get-tuple-element.10.mine), channel_id=1, source_target_pairs={{0,1},{1,2},{2,3},{3,0},{4,5},{5,6},{6,7},{7,4},{8,9},{9,10},{10,1... | collective-permute-start | bytes 9224 | tf_op jit(solution)/shard_map/ppermute | solution.py:137
  11.9 21.8 %copy-start.1 = (f32[1536]{0:T(1024)S(1)}, f32[1536]{0:T(1024)}, u32[]{:S(2)}) copy-start(f32[1536]{0:T(1024)} %param.11) | copy-start | bytes 18436
  11.9 21.8 %copy-start.2 = (s32[12,128]{1,0:T(8,128)S(1)}, s32[12,128]{1,0:T(8,128)}, u32[]{:S(2)}) copy-start(s32[12,128]{1,0:T(8,128)} %get-tuple-element.12.new_leaf) | copy-start | bytes 18436

commit v2 on v1

v2 whole, which is shorter than its diff:
```python
import jax
import jax.numpy as jnp
from jax import lax
from jax.experimental import pallas as pl
from jax.experimental.pallas import tpu as pltpu
from jax.sharding import PartitionSpec as P

B = 256
LEAVES = 8
KIDS = 2 * LEAVES
LANES = 128
GROUP = 32
LOW = jnp.float8_e4m3fn
VMEM = pl.BlockSpec(memory_space=pltpu.VMEM)
SMALL = pltpu.CompilerParams(vmem_limit_bytes=16 << 20)
SMEM = pl.BlockSpec(memory_space=pltpu.SMEM)


def split_kernel(bins, leaf, features, cutoffs, part, packed, cells, rows, leaves, wanted, limits, sems):
    width, length = bins.shape
    blocks = length // LANES
    copies = [(features, wanted), (cutoffs, limits), (leaf, leaves)]
    copies += [(bins.at[pl.ds(top, 8), :], cells.at[pl.ds(top, 8), :]) for top in range(0, width, 8)]
    copies = [pltpu.make_async_copy(source, target, sems.at[i]) for i, (source, target) in enumerate(copies)]
    for copy in copies:
        copy.start()
    for copy in copies:
        copy.wait()
    for top in range(0, width, 8):
        for k in range(blocks):
            rows[pl.ds(top * blocks + k, 8, stride=blocks), :] = cells[top : top + 8, k * LANES : (k + 1) * LANES]
    first = lax.axis_index("feat") * width
    code = jnp.zeros((blocks, LANES), jnp.int32)
    for slot in range(LEAVES):
        local = wanted[slot] - first
        here = ((local >= 0) & (local < width)).astype(jnp.int32)
        chosen = rows[pl.ds(jnp.clip(local, 0, width - 1) * blocks, blocks), :]
        child = (2 * slot + (chosen > limits[slot]).astype(jnp.int32)) * here
        code = jnp.where(leaves[...] == slot, child, code)
    part[...] = code.astype(jnp.float32).astype(jnp.bfloat16)
    owners, each, _ = packed.shape
    for owner in range(owners):
        packed[owner] = rows[owner * each : (owner + 1) * each, :].astype(jnp.float32).astype(jnp.bfloat16)


def fill_kernel(count, packed, gradients, hessians, mine, one, two, three, send, code, stage):
    owners, each, _ = packed.shape
    blocks = mine.shape[0]
    total = sum(x[...].astype(jnp.float32) for x in (mine, one, two, three))
    code[...] = total.astype(jnp.int32)
    spot = lax.broadcasted_iota(jnp.int32, (blocks, LANES), 0) * LANES
    spot = spot + lax.broadcasted_iota(jnp.int32, (blocks, LANES), 1)
    live = spot < count[0]
    stage[0:blocks, :] = jnp.where(live, gradients[...].astype(jnp.float32), 0.0)
    stage[blocks : 2 * blocks, :] = jnp.where(live, hessians[...].astype(jnp.float32), 0.0)
    stage[2 * blocks : 3 * blocks, :] = total
    used = (count[0] + LANES - 1) // LANES
    rest = stage.shape[0] - 3 * blocks
    stage[3 * blocks :, :] = jnp.full((rest, LANES), used, jnp.int32).astype(jnp.float32)
    tail = stage[...].astype(jnp.bfloat16)
    for owner in range(owners):
        send[owner, 0:each, :] = packed[owner]
        send[owner, each:, :] = tail


def hist_kernel(recv, code, predictions, hist, new_leaf, new_pred, wide, columns):
    pl.run_scoped(
        lambda *accs: hist_steps(recv, code, predictions, hist, new_leaf, new_pred, wide, columns, accs),
        pltpu.ACC(0)((8 * KIDS, B), jnp.float32),
        pltpu.ACC(1)((8 * KIDS, B), jnp.float32),
    )


def hist_steps(recv, code, predictions, hist, new_leaf, new_pred, wide, columns, accs):
    sources, height, _ = recv.shape
    blocks = code.shape[0]
    each = recv.shape[1]
    for acc in accs:
        pltpu.matmul_pop(acc)
    for s in range(sources):
        wide[s * each : (s + 1) * each, :] = recv[s].astype(jnp.float32)
    place = 0
    for s in range(sources):
        for j in range(5):
            columns[j, pl.ds(place, blocks), :] = wide[s * each + j * blocks : s * each + (j + 1) * blocks, :]
        used = wide[s * each + 5 * blocks : s * each + 5 * blocks + 1, :][0, 0].astype(jnp.int32)
        place = place + used
    for j in range(5):
        columns[j, pl.ds(place, GROUP), :] = jnp.zeros((GROUP, LANES), jnp.float32)
    slots = lax.broadcasted_iota(jnp.int32, (2 * KIDS, LANES), 0).astype(jnp.float32).astype(jnp.bfloat16)
    levels = lax.broadcasted_iota(jnp.int32, (LANES, LANES), 0).astype(jnp.float32).astype(jnp.bfloat16)
    zero = jnp.zeros((), jnp.bfloat16)
    one = jnp.ones((), jnp.bfloat16)

    def spread(row, height):
        return jnp.broadcast_to(row, (height, LANES)).astype(jnp.bfloat16)

    def block(at):
        grad = spread(columns[2, pl.ds(at, 1), :], 2 * KIDS)
        hess = spread(columns[3, pl.ds(at, 1), :], 2 * KIDS)
        child = columns[4, pl.ds(at, 1), :]
        upper = []
        lower = []
        for f in range(2):
            cell = columns[f, pl.ds(at, 1), :]
            high = cell >= LANES
            low = spread(jnp.where(high, cell - LANES, cell), LANES)
            slot = spread(jnp.where(high, child + KIDS, child), 2 * KIDS)
            hit = slot == slots
            upper += [jnp.where(hit, grad, zero), jnp.where(hit, hess, zero)]
            lower.append(jnp.where(low == levels, one, zero))
        return jnp.concatenate(upper, 0), jnp.concatenate(lower, 0)

    def step(i, carry):
        base = i * GROUP
        for k in range(0, GROUP, 2):
            first, second = block(base + k), block(base + k + 1)
            upper = jnp.concatenate([first[0], second[0]], 1)
            lower = jnp.concatenate([first[1], second[1]], 1).astype(LOW)
            unit, slot = (k // 2) % 2, (k // 4) % 2
            pltpu.matmul_push_rhs(lower, staging_register=slot, mxu_index=unit, transpose=True)
            pltpu.matmul_acc_lhs(accs[unit], upper, load_staged_rhs=slot)
        return carry

    lax.fori_loop(0, (place + GROUP - 1) // GROUP, step, 0)
    total = pltpu.matmul_pop(accs[0]) + pltpu.matmul_pop(accs[1])
    for f in range(2):
        mine = total[f * 4 * KIDS : (f + 1) * 4 * KIDS, f * LANES : (f + 1) * LANES]
        for kind in range(2):
            for high in range(2):
                top = (kind * 2 + high) * KIDS
                hist[f, kind, :, high * LANES : (high + 1) * LANES] = mine[top : top + KIDS, :]
        if f == 0:
            sums = [jnp.sum(mine[top : top + KIDS, :] + mine[top + KIDS : top + 2 * KIDS, :], 1, keepdims=True) for top in (0, 2 * KIDS)]
    value = -sums[0] / (sums[1] + 1.0)
    kids = code[...]
    new_leaf[...] = kids
    gained = jnp.zeros(kids.shape, jnp.float32)
    for c in range(KIDS):
        gained = jnp.where(kids == c, jnp.broadcast_to(value[c : c + 1, :], kids.shape), gained)
    new_pred[...] = predictions[...] + 0.5 * gained


def body(bins, gradients, hessians, predictions, leaf, split_feature, split_bin, row_counts):
    width, length = bins.shape
    blocks = length // LANES
    owners = lax.axis_size("rows")
    feats = lax.axis_size("feat")
    each = width // owners * blocks
    shape = jax.ShapeDtypeStruct
    tall = lambda x: x.reshape(blocks, LANES)
    here = pl.BlockSpec(memory_space=pltpu.HBM)
    height = each + 3 * blocks + 4
    part, packed = pl.pallas_call(
        split_kernel,
        out_shape=(shape((blocks, LANES), jnp.bfloat16), shape((owners, each, LANES), jnp.bfloat16)),
        in_specs=[here] * 4,
        out_specs=(VMEM, VMEM),
        scratch_shapes=[
            pltpu.VMEM((width, length), jnp.int32),
            pltpu.VMEM((width * blocks, LANES), jnp.int32),
            pltpu.VMEM((blocks, LANES), jnp.int32),
            pltpu.SMEM((LEAVES,), jnp.int32),
            pltpu.SMEM((LEAVES,), jnp.int32),
            pltpu.SemaphoreType.DMA((3 + width // 8,)),
        ],
        name="split_rows",
        compiler_params=SMALL,
    )(*(pltpu.with_memory_space_constraint(x, pltpu.HBM) for x in (bins, tall(leaf), split_feature, split_bin)))
    others = [lax.ppermute(part, "feat", [(i, (i + s) % feats) for i in range(feats)]) for s in range(1, feats)]
    send, code = pl.pallas_call(
        fill_kernel,
        out_shape=(shape((owners, height, LANES), jnp.bfloat16), shape((blocks, LANES), jnp.int32)),
        in_specs=[SMEM] + [VMEM] * 7,
        out_specs=(VMEM, VMEM),
        scratch_shapes=[pltpu.VMEM((height - each, LANES), jnp.float32)],
        name="fill_messages",
        compiler_params=SMALL,
    )(row_counts, packed, tall(gradients), tall(hessians), part, *others)
    recv = lax.all_to_all(send, "rows", 0, 0, tiled=True)
    hist, new_leaf, new_pred = pl.pallas_call(
        hist_kernel,
        out_shape=(shape((2, 2, KIDS, B), jnp.float32), shape((blocks, LANES), jnp.int32), shape((blocks, LANES), jnp.float32)),
        in_specs=[VMEM] * 3,
        out_specs=(VMEM, VMEM, VMEM),
        scratch_shapes=[
            pltpu.VMEM((owners * height, LANES), jnp.float32),
            pltpu.VMEM((5, owners * blocks + GROUP, LANES), jnp.float32),
        ],
        name="histograms",
        compiler_params=SMALL,
    )(recv, code, tall(predictions))
    return (hist[None], new_leaf.reshape(-1), new_pred.reshape(-1))


def solution(mesh):
    in_specs = (P("feat", "rows"), P("rows"), P("rows"), P("rows"), P("rows"), P(), P(), P("rows"))
    out_specs = (P("feat", "rows", None, None, None), P("rows"), P("rows"))
    return jax.shard_map(body, mesh=mesh, in_specs=in_specs, out_specs=out_specs, check_vma=False)
```

time: 40.4 us -> 34.6 us (0.86); the launches traced: 39.6 us -> 34.4 us
  Pallas kernels: 7.09 us -> 4.36 us
  local copies, waits for them, and re-layouts: 2.37 us -> 0.02 us
    pallas_call x1, Pallas kernels: 5.82 us -> 3.15 us  [body(): pl.pallas_call(hist_kernel, out_shape=(shape((2, 2, KIDS, B), jnp.float32...]
    unnamed x16 -> x6, local copies, waits for them, and re-layouts: 2.37 us -> 0.02 us
    pallas_call x1, Pallas kernels: 0.65 us -> 0.06 us  [body(): pl.pallas_call(fill_kernel, out_shape=(shape((owners, height, LANES), jnp...]
    pallas_call x1, Pallas kernels: 0.61 us -> 1.15 us  [body(): pl.pallas_call(split_kernel, out_shape=(shape((blocks, LANES), jnp.bfloat...]
where the time goes in v2:
time: 34.6 us; the launch traced here: 34.4 us
  blocking collectives  21.7 us (63%)
  starting transfers between devices  4.66 us (13%)
  Pallas kernels  4.36 us (13%)
  waiting for transfers between devices  2.32 us (7%)
  between operations  1.33 us (4%)
    all_to_all x1, blocking collectives, body(): recv = lax.all_to_all(send, 'rows', 0, 0, tiled=True)  21.7 us
    ppermute x3, starting transfers between devices, body(): lax.ppermute(part, 'feat', [(i, (i + s) % feats) for i in range(feats)])  4.66 us
    pallas_call x1, Pallas kernels, body(): pl.pallas_call(hist_kernel, out_shape=(shape((2, 2, KIDS, B), jnp.float32...  3.15 us
    ppermute x3, waiting for transfers between devices, body(): lax.ppermute(part, 'feat', [(i, (i + s) % feats) for i in range(feats)])  2.32 us
    pallas_call x1, Pallas kernels, body(): pl.pallas_call(split_kernel, out_shape=(shape((blocks, LANES), jnp.bfloat...  1.15 us
  transfers between devices with their start and end apart: 3, of which 2 were waited for; matrix products, arithmetic and copies ran while one was open for 0% of the time, Pallas kernels for 0%

profile of v2, /device:TPU:1, one launch (start us, length us, event | category | flops | bytes accessed | tf_op | source)
XLA Modules:
  0.0 34.4 jit_solution(12146583443465444378)
XLA Ops:
  0.6 1.1 %split_rows.1 = (bf16[12,128]{1,0:T(8,128)(2,1)S(1)}, bf16[32,24,128]{2,1,0:T(8,128)(2,1)S(1)}) custom-call(s32[64,1536]{1,0:T(8,128)} %bins.1, s32[12,128]{1,0:T(8,128)} %bitcast.10, s32[8]{0:T(128)} %features.1, s32[8]{0:T(128)} %cutoffs.1), custom_call_target="tpu_custom_call" | custom-call | tf_op jit(solution)/shard_map/split_rows/pallas_call | solution.py:154
  1.8 0.0 copy-start.2
  1.8 0.0 copy-start.1
  1.8 3.6 %collective-permute-start.2 = (bf16[12,128]{1,0:T(8,128)(2,1)S(1)}, bf16[12,128]{1,0:T(8,128)(2,1)S(1)}, u32[]{:S(2)}, u32[]{:S(2)}) collective-permute-start(bf16[12,128]{1,0:T(8,128)(2,1)S(1)} %get-tuple-element.11.mine), channel_id=1, source_target_pairs={{0,3},{1,0},{2,1},{3,2},{4,7},{5,4},{6,5},{7,6},{8,11},{9,8},{10,9... | collective-permute-start | bytes 9224 | tf_op jit(solution)/shard_map/ppermute | solution.py:170
  5.4 0.4 %collective-permute-start.1 = (bf16[12,128]{1,0:T(8,128)(2,1)S(1)}, bf16[12,128]{1,0:T(8,128)(2,1)S(1)}, u32[]{:S(2)}, u32[]{:S(2)}) collective-permute-start(bf16[12,128]{1,0:T(8,128)(2,1)S(1)} %get-tuple-element.11.mine), channel_id=1, source_target_pairs={{0,2},{1,3},{2,0},{3,1},{4,6},{5,7},{6,4},{7,5},{8,10},{9,11},{10,... | collective-permute-start | bytes 9224 | tf_op jit(solution)/shard_map/ppermute | solution.py:170
  5.8 0.7 %collective-permute-start = (bf16[12,128]{1,0:T(8,128)(2,1)S(1)}, bf16[12,128]{1,0:T(8,128)(2,1)S(1)}, u32[]{:S(2)}, u32[]{:S(2)}) collective-permute-start(bf16[12,128]{1,0:T(8,128)(2,1)S(1)} %get-tuple-element.11.mine), channel_id=1, source_target_pairs={{0,1},{1,2},{2,3},{3,0},{4,5},{5,6},{6,7},{7,4},{8,9},{9,10},{10,1... | collective-permute-start | bytes 9224 | tf_op jit(solution)/shard_map/ppermute | solution.py:170
  7.1 0.0 collective-permute-done.2.three
  7.1 2.3 %collective-permute-done.1.two = bf16[12,128]{1,0:T(8,128)(2,1)S(1)} collective-permute-done((bf16[12,128]{1,0:T(8,128)(2,1)S(1)}, bf16[12,128]{1,0:T(8,128)(2,1)S(1)}, u32[]{:S(2)}, u32[]{:S(2)}) %collective-permute-start.1) | collective-permute-done | bytes 3104 | tf_op jit(solution)/shard_map/ppermute | solution.py:170
  9.4 0.1 collective-permute-done.one
  9.4 0.0 copy-done.2
  9.5 0.0 copy-done.1
  9.5 0.1 fill_messages.1
  9.5 0.0 copy-start
  9.5 21.7 %all_to_all.5.recv = bf16[32,64,128]{2,1,0:T(8,128)(2,1)S(1)} all-to-all(bf16[32,64,128]{2,1,0:T(8,128)(2,1)S(1)} %get-tuple-element.12), channel_id=1, replica_groups=mesh['rows'=32,'feat'=4] {'rows'}, dimensions={0} | all-to-all | bytes 1048576 | tf_op jit(solution)/shard_map/all_to_all | solution.py:180
  31.2 0.0 copy-done
  31.2 3.1 %histograms.1 = (f32[2,2,16,256]{3,2,1,0:T(8,128)}, s32[12,128]{1,0:T(8,128)}, f32[12,128]{1,0:T(8,128)}) custom-call(bf16[32,64,128]{2,1,0:T(8,128)(2,1)S(1)} %all_to_all.5.recv, s32[12,128]{1,0:T(8,128)S(1)} %get-tuple-element.13.code, f32[12,128]{1,0:T(8,128)S(1)} %bitcast.7), custom_call_target="tpu_custom_call" | custom-call | tf_op jit(solution)/shard_map/histograms/pallas_call | solution.py:181
Async XLA Ops:
  1.8 7.7 %copy-start.2 = (bf16[1536]{0:T(1024)(128)(2,1)S(1)}, bf16[1536]{0:T(1024)(128)(2,1)}, u32[]{:S(2)}) copy-start(bf16[1536]{0:T(1024)(128)(2,1)} %param.10) | copy-start | bytes 9220
  1.8 7.7 %copy-start.1 = (bf16[1536]{0:T(1024)(128)(2,1)S(1)}, bf16[1536]{0:T(1024)(128)(2,1)}, u32[]{:S(2)}) copy-start(bf16[1536]{0:T(1024)(128)(2,1)} %param.9) | copy-start | bytes 9220
  1.8 5.3 %collective-permute-start.2 = (bf16[12,128]{1,0:T(8,128)(2,1)S(1)}, bf16[12,128]{1,0:T(8,128)(2,1)S(1)}, u32[]{:S(2)}, u32[]{:S(2)}) collective-permute-start(bf16[12,128]{1,0:T(8,128)(2,1)S(1)} %get-tuple-element.11.mine), channel_id=1, source_target_pairs={{0,3},{1,0},{2,1},{3,2},{4,7},{5,4},{6,5},{7,6},{8,11},{9,8},{10,9... | collective-permute-start | bytes 9224 | tf_op jit(solution)/shard_map/ppermute | solution.py:170
  5.4 4.0 %collective-permute-start.1 = (bf16[12,128]{1,0:T(8,128)(2,1)S(1)}, bf16[12,128]{1,0:T(8,128)(2,1)S(1)}, u32[]{:S(2)}, u32[]{:S(2)}) collective-permute-start(bf16[12,128]{1,0:T(8,128)(2,1)S(1)} %get-tuple-element.11.mine), channel_id=1, source_target_pairs={{0,2},{1,3},{2,0},{3,1},{4,6},{5,7},{6,4},{7,5},{8,10},{9,11},{10,... | collective-permute-start | bytes 9224 | tf_op jit(solution)/shard_map/ppermute | solution.py:170
  5.8 3.7 %collective-permute-start = (bf16[12,128]{1,0:T(8,128)(2,1)S(1)}, bf16[12,128]{1,0:T(8,128)(2,1)S(1)}, u32[]{:S(2)}, u32[]{:S(2)}) collective-permute-start(bf16[12,128]{1,0:T(8,128)(2,1)S(1)} %get-tuple-element.11.mine), channel_id=1, source_target_pairs={{0,1},{1,2},{2,3},{3,0},{4,5},{5,6},{6,7},{7,4},{8,9},{9,10},{10,1... | collective-permute-start | bytes 9224 | tf_op jit(solution)/shard_map/ppermute | solution.py:170
  9.5 21.7 %copy-start = (f32[1536]{0:T(1024)S(1)}, f32[1536]{0:T(1024)}, u32[]{:S(2)}) copy-start(f32[1536]{0:T(1024)} %param.11) | copy-start | bytes 18436

commit v3 on v2

--- a/solution.py
+++ b/solution.py
@@ -167,7 +167,7 @@
         name="split_rows",
         compiler_params=SMALL,
     )(*(pltpu.with_memory_space_constraint(x, pltpu.HBM) for x in (bins, tall(leaf), split_feature, split_bin)))
-    others = [lax.ppermute(part, "feat", [(i, (i + s) % feats) for i in range(feats)]) for s in range(1, feats)]
+    others = [lax.ppermute(part, "feat", [(i, (i + s) % feats) for i in range(feats)]) for s in (3, 1, 2)]
     send, code = pl.pallas_call(
         fill_kernel,
         out_shape=(shape((owners, height, LANES), jnp.bfloat16), shape((blocks, LANES), jnp.int32)),

time: 34.6 us -> 34 us (0.983)
  waiting for transfers between devices: 2.32 us -> 0.33 us
  starting transfers between devices: 4.66 us -> 6.49 us
    ppermute x3, waiting for transfers between devices: 2.32 us -> 0.33 us  [body(): lax.ppermute(part, 'feat', [(i, (i + s) % feats) for i in range(feats)])]
    ppermute x3, starting transfers between devices: 4.66 us -> 6.49 us  [body(): lax.ppermute(part, 'feat', [(i, (i + s) % feats) for i in range(feats)])]
  transfers between devices with their start and end apart: 3 -> 3, of which waited for: 2 -> 1; matrix products, arithmetic and copies ran while one was open for 0% -> 0% of each run, Pallas kernels for 0% -> 0%
where the time goes in v3:
time: 34 us
  blocking collectives  21.4 us (63%)
  starting transfers between devices  6.49 us (19%)
  Pallas kernels  4.36 us (13%)
  between operations  1.34 us (4%)
    all_to_all x1, blocking collectives, body(): recv = lax.all_to_all(send, 'rows', 0, 0, tiled=True)  21.4 us
    ppermute x3, starting transfers between devices, body(): lax.ppermute(part, 'feat', [(i, (i + s) % feats) for i in range(feats)])  6.49 us
    pallas_call x1, Pallas kernels, body(): pl.pallas_call(hist_kernel, out_shape=(shape((2, 2, KIDS, B), jnp.float32...  3.15 us
    pallas_call x1, Pallas kernels, body(): pl.pallas_call(split_kernel, out_shape=(shape((blocks, LANES), jnp.bfloat...  1.15 us
  transfers between devices with their start and end apart: 3, of which 1 were waited for; matrix products, arithmetic and copies ran while one was open for 0% of the time, Pallas kernels for 0%

profile of v3, /device:TPU:1, one launch (start us, length us, event | category | flops | bytes accessed | tf_op | source)
XLA Modules:
  0.0 34.0 jit_solution(10327053131869742917)
XLA Ops:
  0.6 1.1 %split_rows.1 = (bf16[12,128]{1,0:T(8,128)(2,1)S(1)}, bf16[32,24,128]{2,1,0:T(8,128)(2,1)S(1)}) custom-call(s32[64,1536]{1,0:T(8,128)} %bins.1, s32[12,128]{1,0:T(8,128)} %bitcast.10, s32[8]{0:T(128)} %features.1, s32[8]{0:T(128)} %cutoffs.1), custom_call_target="tpu_custom_call" | custom-call | tf_op jit(solution)/shard_map/split_rows/pallas_call | solution.py:154
  1.8 0.0 copy-start.2
  1.8 0.0 copy-start.1
  1.8 3.8 %collective-permute-start.2 = (bf16[12,128]{1,0:T(8,128)(2,1)S(1)}, bf16[12,128]{1,0:T(8,128)(2,1)S(1)}, u32[]{:S(2)}, u32[]{:S(2)}) collective-permute-start(bf16[12,128]{1,0:T(8,128)(2,1)S(1)} %get-tuple-element.11.mine), channel_id=1, source_target_pairs={{0,2},{1,3},{2,0},{3,1},{4,6},{5,7},{6,4},{7,5},{8,10},{9,11},{10,... | collective-permute-start | bytes 9224 | tf_op jit(solution)/shard_map/ppermute | solution.py:170
  5.6 0.4 %collective-permute-start.1 = (bf16[12,128]{1,0:T(8,128)(2,1)S(1)}, bf16[12,128]{1,0:T(8,128)(2,1)S(1)}, u32[]{:S(2)}, u32[]{:S(2)}) collective-permute-start(bf16[12,128]{1,0:T(8,128)(2,1)S(1)} %get-tuple-element.11.mine), channel_id=1, source_target_pairs={{0,1},{1,2},{2,3},{3,0},{4,5},{5,6},{6,7},{7,4},{8,9},{9,10},{10,1... | collective-permute-start | bytes 9224 | tf_op jit(solution)/shard_map/ppermute | solution.py:170
  6.0 2.3 %collective-permute-start = (bf16[12,128]{1,0:T(8,128)(2,1)S(1)}, bf16[12,128]{1,0:T(8,128)(2,1)S(1)}, u32[]{:S(2)}, u32[]{:S(2)}) collective-permute-start(bf16[12,128]{1,0:T(8,128)(2,1)S(1)} %get-tuple-element.11.mine), channel_id=1, source_target_pairs={{0,3},{1,0},{2,1},{3,2},{4,7},{5,4},{6,5},{7,6},{8,11},{9,8},{10,9... | collective-permute-start | bytes 9224 | tf_op jit(solution)/shard_map/ppermute | solution.py:170
  8.9 0.0 collective-permute-done.2.three
  9.0 0.3 collective-permute-done.1.two
  9.3 0.0 collective-permute-done.one
  9.3 0.0 copy-done.2
  9.3 0.0 copy-done.1
  9.3 0.1 fill_messages.1
  9.4 0.0 copy-start
  9.4 21.4 %all_to_all.5.recv = bf16[32,64,128]{2,1,0:T(8,128)(2,1)S(1)} all-to-all(bf16[32,64,128]{2,1,0:T(8,128)(2,1)S(1)} %get-tuple-element.12), channel_id=1, replica_groups=mesh['rows'=32,'feat'=4] {'rows'}, dimensions={0} | all-to-all | bytes 1048576 | tf_op jit(solution)/shard_map/all_to_all | solution.py:180
  30.8 0.0 copy-done
  30.8 3.2 %histograms.1 = (f32[2,2,16,256]{3,2,1,0:T(8,128)}, s32[12,128]{1,0:T(8,128)}, f32[12,128]{1,0:T(8,128)}) custom-call(bf16[32,64,128]{2,1,0:T(8,128)(2,1)S(1)} %all_to_all.5.recv, s32[12,128]{1,0:T(8,128)S(1)} %get-tuple-element.13.code, f32[12,128]{1,0:T(8,128)S(1)} %bitcast.7), custom_call_target="tpu_custom_call" | custom-call | tf_op jit(solution)/shard_map/histograms/pallas_call | solution.py:181
Async XLA Ops:
  1.8 7.5 %copy-start.2 = (bf16[1536]{0:T(1024)(128)(2,1)S(1)}, bf16[1536]{0:T(1024)(128)(2,1)}, u32[]{:S(2)}) copy-start(bf16[1536]{0:T(1024)(128)(2,1)} %param.10) | copy-start | bytes 9220
  1.8 7.5 %copy-start.1 = (bf16[1536]{0:T(1024)(128)(2,1)S(1)}, bf16[1536]{0:T(1024)(128)(2,1)}, u32[]{:S(2)}) copy-start(bf16[1536]{0:T(1024)(128)(2,1)} %param.9) | copy-start | bytes 9220
  1.8 7.1 %collective-permute-start.2 = (bf16[12,128]{1,0:T(8,128)(2,1)S(1)}, bf16[12,128]{1,0:T(8,128)(2,1)S(1)}, u32[]{:S(2)}, u32[]{:S(2)}) collective-permute-start(bf16[12,128]{1,0:T(8,128)(2,1)S(1)} %get-tuple-element.11.mine), channel_id=1, source_target_pairs={{0,2},{1,3},{2,0},{3,1},{4,6},{5,7},{6,4},{7,5},{8,10},{9,11},{10,... | collective-permute-start | bytes 9224 | tf_op jit(solution)/shard_map/ppermute | solution.py:170
  5.6 3.7 %collective-permute-start.1 = (bf16[12,128]{1,0:T(8,128)(2,1)S(1)}, bf16[12,128]{1,0:T(8,128)(2,1)S(1)}, u32[]{:S(2)}, u32[]{:S(2)}) collective-permute-start(bf16[12,128]{1,0:T(8,128)(2,1)S(1)} %get-tuple-element.11.mine), channel_id=1, source_target_pairs={{0,1},{1,2},{2,3},{3,0},{4,5},{5,6},{6,7},{7,4},{8,9},{9,10},{10,1... | collective-permute-start | bytes 9224 | tf_op jit(solution)/shard_map/ppermute | solution.py:170
  6.0 3.3 %collective-permute-start = (bf16[12,128]{1,0:T(8,128)(2,1)S(1)}, bf16[12,128]{1,0:T(8,128)(2,1)S(1)}, u32[]{:S(2)}, u32[]{:S(2)}) collective-permute-start(bf16[12,128]{1,0:T(8,128)(2,1)S(1)} %get-tuple-element.11.mine), channel_id=1, source_target_pairs={{0,3},{1,0},{2,1},{3,2},{4,7},{5,4},{6,5},{7,6},{8,11},{9,8},{10,9... | collective-permute-start | bytes 9224 | tf_op jit(solution)/shard_map/ppermute | solution.py:170
  9.4 21.4 %copy-start = (f32[1536]{0:T(1024)S(1)}, f32[1536]{0:T(1024)}, u32[]{:S(2)}) copy-start(f32[1536]{0:T(1024)} %param.11) | copy-start | bytes 18436

commit v4 on v3

--- a/solution.py
+++ b/solution.py
@@ -9,7 +9,7 @@
 LEAVES = 8
 KIDS = 2 * LEAVES
 LANES = 128
-GROUP = 32
+GROUP = 16
 LOW = jnp.float8_e4m3fn
 VMEM = pl.BlockSpec(memory_space=pltpu.VMEM)
 SMALL = pltpu.CompilerParams(vmem_limit_bytes=16 << 20)
@@ -39,52 +39,50 @@
         code = jnp.where(leaves[...] == slot, child, code)
     part[...] = code.astype(jnp.float32).astype(jnp.bfloat16)
     owners, each, _ = packed.shape
+    half = blocks // 2
     for owner in range(owners):
-        packed[owner] = rows[owner * each : (owner + 1) * each, :].astype(jnp.float32).astype(jnp.bfloat16)
+        order = [(parity, top) for parity in (owner % 2, 1 - owner % 2) for top in range(owner * each, (owner + 1) * each, blocks)]
+        picked = [rows[pl.ds(top + parity, half, stride=2), :].astype(jnp.float32) for parity, top in order]
+        packed[owner] = jnp.concatenate(picked, 0).astype(jnp.bfloat16)
 
 
 def fill_kernel(count, packed, gradients, hessians, mine, one, two, three, send, code, stage):
     owners, each, _ = packed.shape
     blocks = mine.shape[0]
+    half = blocks // 2
     total = sum(x[...].astype(jnp.float32) for x in (mine, one, two, three))
     code[...] = total.astype(jnp.int32)
     spot = lax.broadcasted_iota(jnp.int32, (blocks, LANES), 0) * LANES
     spot = spot + lax.broadcasted_iota(jnp.int32, (blocks, LANES), 1)
     live = spot < count[0]
+    used = (count[0] + LANES - 1) // LANES
     stage[0:blocks, :] = jnp.where(live, gradients[...].astype(jnp.float32), 0.0)
     stage[blocks : 2 * blocks, :] = jnp.where(live, hessians[...].astype(jnp.float32), 0.0)
     stage[2 * blocks : 3 * blocks, :] = total
-    used = (count[0] + LANES - 1) // LANES
-    rest = stage.shape[0] - 3 * blocks
-    stage[3 * blocks :, :] = jnp.full((rest, LANES), used, jnp.int32).astype(jnp.float32)
-    tail = stage[...].astype(jnp.bfloat16)
+    stage[3 * blocks :, :] = jnp.full((blocks, LANES), used, jnp.int32).astype(jnp.float32)
+    tails = []
+    for core in range(2):
+        rows = [stage[pl.ds(j * blocks + core, half, stride=2), :] for j in range(4)]
+        tails.append(jnp.concatenate(rows, 0).astype(jnp.bfloat16))
     for owner in range(owners):
         send[owner, 0:each, :] = packed[owner]
-        send[owner, each:, :] = tail
-
-
-def hist_kernel(recv, code, predictions, hist, new_leaf, new_pred, wide, columns):
-    pl.run_scoped(
-        lambda *accs: hist_steps(recv, code, predictions, hist, new_leaf, new_pred, wide, columns, accs),
-        pltpu.ACC(0)((8 * KIDS, B), jnp.float32),
-        pltpu.ACC(1)((8 * KIDS, B), jnp.float32),
-    )
-
-
-def hist_steps(recv, code, predictions, hist, new_leaf, new_pred, wide, columns, accs):
-    sources, height, _ = recv.shape
-    blocks = code.shape[0]
-    each = recv.shape[1]
+        send[owner, each:, :] = tails[owner % 2]
+
+
+def accumulate(cells, first, weights, counts, wide, columns, accs):
+    sources, each, _ = cells.shape
+    half = each // 8
     for acc in accs:
         pltpu.matmul_pop(acc)
-    for s in range(sources):
-        wide[s * each : (s + 1) * each, :] = recv[s].astype(jnp.float32)
     place = 0
     for s in range(sources):
-        for j in range(5):
-            columns[j, pl.ds(place, blocks), :] = wide[s * each + j * blocks : s * each + (j + 1) * blocks, :]
-        used = wide[s * each + 5 * blocks : s * each + 5 * blocks + 1, :][0, 0].astype(jnp.int32)
-        place = place + used
+        wide[s * each : s * each + each // 2, :] = cells[s, : each // 2, :].astype(jnp.float32)
+        wide[s * each + each // 2 : (s + 1) * each, :] = weights[s, each // 2 :, :].astype(jnp.float32)
+    for s in range(sources):
+        for j, top in enumerate((first, first + half, 4 * half, 5 * half, 6 * half)):
+            columns[j, pl.ds(place, half), :] = wide[s * each + top : s * each + top + half, :]
+        used = wide[s * each + 7 * half : s * each + 7 * half + 1, :][0, 0].astype(jnp.int32)
+        place = place + counts(used)
     for j in range(5):
         columns[j, pl.ds(place, GROUP), :] = jnp.zeros((GROUP, LANES), jnp.float32)
     slots = lax.broadcasted_iota(jnp.int32, (2 * KIDS, LANES), 0).astype(jnp.float32).astype(jnp.bfloat16)
@@ -123,22 +121,50 @@
         return carry
 
     lax.fori_loop(0, (place + GROUP - 1) // GROUP, step, 0)
-    total = pltpu.matmul_pop(accs[0]) + pltpu.matmul_pop(accs[1])
-    for f in range(2):
-        mine = total[f * 4 * KIDS : (f + 1) * 4 * KIDS, f * LANES : (f + 1) * LANES]
-        for kind in range(2):
-            for high in range(2):
-                top = (kind * 2 + high) * KIDS
-                hist[f, kind, :, high * LANES : (high + 1) * LANES] = mine[top : top + KIDS, :]
-        if f == 0:
-            sums = [jnp.sum(mine[top : top + KIDS, :] + mine[top + KIDS : top + 2 * KIDS, :], 1, keepdims=True) for top in (0, 2 * KIDS)]
-    value = -sums[0] / (sums[1] + 1.0)
-    kids = code[...]
-    new_leaf[...] = kids
-    gained = jnp.zeros(kids.shape, jnp.float32)
-    for c in range(KIDS):
-        gained = jnp.where(kids == c, jnp.broadcast_to(value[c : c + 1, :], kids.shape), gained)
-    new_pred[...] = predictions[...] + 0.5 * gained
+    return pltpu.matmul_pop(accs[0]) + pltpu.matmul_pop(accs[1])
+
+
+def scoped(steps):
+    pl.run_scoped(
+        lambda *accs: steps(accs),
+        pltpu.ACC(0)((8 * KIDS, B), jnp.float32),
+        pltpu.ACC(1)((8 * KIDS, B), jnp.float32),
+    )
+
+
+def first_kernel(recv, partial, wide, columns):
+    core = lax.rem(lax.axis_index("rows"), 2)
+
+    def steps(accs):
+        total = accumulate(recv, 0, recv, lambda used: (used + 1 - core) >> 1, wide, columns, accs)
+        for f in range(2):
+            partial[f] = total[f * 4 * KIDS : (f + 1) * 4 * KIDS, f * LANES : (f + 1) * LANES]
+
+    scoped(steps)
+
+
+def last_kernel(recv, other, partial, code, predictions, hist, new_leaf, new_pred, wide, columns):
+    core = lax.rem(lax.axis_index("rows"), 2)
+
+    def steps(accs):
+        total = accumulate(recv, recv.shape[1] // 4, other, lambda used: (used + core) >> 1, wide, columns, accs)
+        for f in range(2):
+            mine = partial[f] + total[f * 4 * KIDS : (f + 1) * 4 * KIDS, f * LANES : (f + 1) * LANES]
+            for kind in range(2):
+                for high in range(2):
+                    top = (kind * 2 + high) * KIDS
+                    hist[f, kind, :, high * LANES : (high + 1) * LANES] = mine[top : top + KIDS, :]
+            if f == 0:
+                sums = [jnp.sum(mine[top : top + KIDS, :] + mine[top + KIDS : top + 2 * KIDS, :], 1, keepdims=True) for top in (0, 2 * KIDS)]
+        value = -sums[0] / (sums[1] + 1.0)
+        leaves = code[...]
+        new_leaf[...] = leaves
+        gained = jnp.zeros(leaves.shape, jnp.float32)
+        for c in range(KIDS):
+            gained = jnp.where(leaves == c, jnp.broadcast_to(value[c : c + 1, :], leaves.shape), gained)
+        new_pred[...] = predictions[...] + 0.5 * gained
+
+    scoped(steps)
 
 
 def body(bins, gradients, hessians, predictions, leaf, split_feature, split_bin, row_counts):
@@ -150,7 +176,9 @@
     shape = jax.ShapeDtypeStruct
     tall = lambda x: x.reshape(blocks, LANES)
     here = pl.BlockSpec(memory_space=pltpu.HBM)
-    height = each + 3 * blocks + 4
+    height = 2 * each
+    wide = pltpu.VMEM((owners * height, LANES), jnp.float32)
+    columns = pltpu.VMEM((5, owners * blocks // 2 + GROUP, LANES), jnp.float32)
     part, packed = pl.pallas_call(
         split_kernel,
         out_shape=(shape((blocks, LANES), jnp.bfloat16), shape((owners, each, LANES), jnp.bfloat16)),
@@ -173,23 +201,31 @@
         out_shape=(shape((owners, height, LANES), jnp.bfloat16), shape((blocks, LANES), jnp.int32)),
         in_specs=[SMEM] + [VMEM] * 7,
         out_specs=(VMEM, VMEM),
-        scratch_shapes=[pltpu.VMEM((height - each, LANES), jnp.float32)],
+        scratch_shapes=[pltpu.VMEM((4 * blocks, LANES), jnp.float32)],
         name="fill_messages",
         compiler_params=SMALL,
     )(row_counts, packed, tall(gradients), tall(hessians), part, *others)
     recv = lax.all_to_all(send, "rows", 0, 0, tiled=True)
+    other = lax.ppermute(recv, "rows", [(i, i ^ 1) for i in range(owners)])
+    partial = pl.pallas_call(
+        first_kernel,
+        out_shape=shape((2, 4 * KIDS, LANES), jnp.float32),
+        in_specs=[VMEM],
+        out_specs=VMEM,
+        scratch_shapes=[wide, columns],
+        name="first_half",
+        cost_estimate=pl.CostEstimate(flops=1 << 30, transcendentals=0, bytes_accessed=1 << 20),
+        compiler_params=SMALL,
+    )(recv)
     hist, new_leaf, new_pred = pl.pallas_call(
-        hist_kernel,
+        last_kernel,
         out_shape=(shape((2, 2, KIDS, B), jnp.float32), shape((blocks, LANES), jnp.int32), shape((blocks, LANES), jnp.float32)),
-        in_specs=[VMEM] * 3,
+        in_specs=[VMEM] * 5,
         out_specs=(VMEM, VMEM, VMEM),
-        scratch_shapes=[
-            pltpu.VMEM((owners * height, LANES), jnp.float32),
-            pltpu.VMEM((5, owners * blocks + GROUP, LANES), jnp.float32),
-        ],
+        scratch_shapes=[wide, columns],
         name="histograms",
         compiler_params=SMALL,
-    )(recv, code, tall(predictions))
+    )(recv, other, partial, code, tall(predictions))
     return (hist[None], new_leaf.reshape(-1), new_pred.reshape(-1))
 
 

time: 34 us -> 33.6 us (0.988)
  blocking collectives: 21.4 us -> 20.1 us
  Pallas kernels: 4.36 us -> 4.95 us
    all_to_all x1, blocking collectives: 21.4 us -> 20.1 us  [body(): recv = lax.all_to_all(send, 'rows', 0, 0, tiled=True)]
    pallas_call x1 -> x2, Pallas kernels: 3.15 us -> 3.73 us  [the longest x1 2.2 us: body(): pl.pallas_call(last_kernel, out_shape=(shape((2, 2, KIDS, B), jnp.float32...]
  transfers between devices with their start and end apart: 3 -> 4, of which waited for: 1 -> 2; matrix products, arithmetic and copies ran while one was open for 0% -> 0% of each run, Pallas kernels for 0% -> 5%
where the time goes in v4:
time: 33.6 us; the launch traced here: 33.4 us
  blocking collectives  20.1 us (60%)
  starting transfers between devices  6.49 us (19%)
  Pallas kernels  4.95 us (15%)
  between operations  1.34 us (4%)
  waiting for transfers between devices  0.52 us (2%)
    all_to_all x1, blocking collectives, body(): recv = lax.all_to_all(send, 'rows', 0, 0, tiled=True)  20.1 us
    ppermute x3, starting transfers between devices, body(): lax.ppermute(part, 'feat', [(i, (i + s) % feats) for i in range(feats)])  6.49 us
    pallas_call x1, Pallas kernels, body(): pl.pallas_call(last_kernel, out_shape=(shape((2, 2, KIDS, B), jnp.float32...  2.2 us
    pallas_call x1, Pallas kernels, body(): pl.pallas_call(first_kernel, out_shape=shape((2, 4 * KIDS, LANES), jnp.fl...  1.53 us
    pallas_call x1, Pallas kernels, body(): pl.pallas_call(split_kernel, out_shape=(shape((blocks, LANES), jnp.bfloat...  1.18 us
  transfers between devices with their start and end apart: 4, of which 2 were waited for; matrix products, arithmetic and copies ran while one was open for 0% of the time, Pallas kernels for 5%

profile of v4, /device:TPU:1, one launch (start us, length us, event | category | flops | bytes accessed | tf_op | source)
XLA Modules:
  0.0 33.4 jit_solution(1090075224130521618)
XLA Ops:
  0.6 1.2 %split_rows.1 = (bf16[12,128]{1,0:T(8,128)(2,1)S(1)}, bf16[32,24,128]{2,1,0:T(8,128)(2,1)S(1)}) custom-call(s32[64,1536]{1,0:T(8,128)} %bins.1, s32[12,128]{1,0:T(8,128)} %bitcast.10, s32[8]{0:T(128)} %features.1, s32[8]{0:T(128)} %cutoffs.1), custom_call_target="tpu_custom_call" | custom-call | tf_op jit(solution)/shard_map/split_rows/pallas_call | solution.py:182
  1.8 0.0 copy-start.2
  1.8 0.0 copy-start.1
  1.8 3.8 %collective-permute-start.2 = (bf16[12,128]{1,0:T(8,128)(2,1)S(1)}, bf16[12,128]{1,0:T(8,128)(2,1)S(1)}, u32[]{:S(2)}, u32[]{:S(2)}) collective-permute-start(bf16[12,128]{1,0:T(8,128)(2,1)S(1)} %get-tuple-element.11.mine), channel_id=1, source_target_pairs={{0,2},{1,3},{2,0},{3,1},{4,6},{5,7},{6,4},{7,5},{8,10},{9,11},{10,... | collective-permute-start | bytes 9224 | tf_op jit(solution)/shard_map/ppermute | solution.py:198
  5.7 0.4 %collective-permute-start.1 = (bf16[12,128]{1,0:T(8,128)(2,1)S(1)}, bf16[12,128]{1,0:T(8,128)(2,1)S(1)}, u32[]{:S(2)}, u32[]{:S(2)}) collective-permute-start(bf16[12,128]{1,0:T(8,128)(2,1)S(1)} %get-tuple-element.11.mine), channel_id=1, source_target_pairs={{0,1},{1,2},{2,3},{3,0},{4,5},{5,6},{6,7},{7,4},{8,9},{9,10},{10,1... | collective-permute-start | bytes 9224 | tf_op jit(solution)/shard_map/ppermute | solution.py:198
  6.1 2.3 %collective-permute-start = (bf16[12,128]{1,0:T(8,128)(2,1)S(1)}, bf16[12,128]{1,0:T(8,128)(2,1)S(1)}, u32[]{:S(2)}, u32[]{:S(2)}) collective-permute-start(bf16[12,128]{1,0:T(8,128)(2,1)S(1)} %get-tuple-element.11.mine), channel_id=1, source_target_pairs={{0,3},{1,0},{2,1},{3,2},{4,7},{5,4},{6,5},{7,6},{8,11},{9,8},{10,9... | collective-permute-start | bytes 9224 | tf_op jit(solution)/shard_map/ppermute | solution.py:198
  9.0 0.0 collective-permute-done.2.three
  9.0 0.3 collective-permute-done.1.two
  9.3 0.0 collective-permute-done.one
  9.3 0.0 copy-done.2
  9.3 0.0 copy-done.1
  9.4 20.1 %all_to_all.5.recv = bf16[32,48,128]{2,1,0:T(8,128)(2,1)S(1)} all-to-all(bf16[32,48,128]{2,1,0:T(8,128)(2,1)S(1)} %get-tuple-element.12), channel_id=1, replica_groups=mesh['rows'=32,'feat'=4] {'rows'}, dimensions={0} | all-to-all | bytes 786432 | tf_op jit(solution)/shard_map/all_to_all | solution.py:208
  29.5 0.0 collective-permute-start.3
  29.5 0.0 copy-start
  29.5 1.5 %first_half.1.partial = f32[2,64,128]{2,1,0:T(8,128)S(1)} custom-call(bf16[32,48,128]{2,1,0:T(8,128)(2,1)S(1)} %all_to_all.5.recv), custom_call_target="tpu_custom_call" | custom-call | flops 1073741824 | bytes 1048576 | tf_op jit(solution)/shard_map/first_half/pallas_call | solution.py:210
  31.0 0.2 collective-permute-done.3.other
  31.2 0.0 copy-done
  31.2 2.2 %histograms.1 = (f32[2,2,16,256]{3,2,1,0:T(8,128)}, s32[12,128]{1,0:T(8,128)}, f32[12,128]{1,0:T(8,128)}) custom-call(bf16[32,48,128]{2,1,0:T(8,128)(2,1)S(1)} %all_to_all.5.recv, bf16[32,48,128]{2,1,0:T(8,128)(2,1)S(1)} %collective-permute-done.3.other, f32[2,64,128]{2,1,0:T(8,128)S(1)} %first_half.1.partial, s32[12,128]{1,0:T(8,128)S(1)} %get-tuple-element.13.code, ...), custom_call_target="tpu_custom_call" | custom-call | tf_op jit(solution)/shard_map/histograms/pallas_call | solution.py:220
  (1 shorter events, 0.0 us)
Async XLA Ops:
  1.8 7.5 %copy-start.2 = (bf16[1536]{0:T(1024)(128)(2,1)S(1)}, bf16[1536]{0:T(1024)(128)(2,1)}, u32[]{:S(2)}) copy-start(bf16[1536]{0:T(1024)(128)(2,1)} %param.10) | copy-start | bytes 9220
  1.8 7.5 %copy-start.1 = (bf16[1536]{0:T(1024)(128)(2,1)S(1)}, bf16[1536]{0:T(1024)(128)(2,1)}, u32[]{:S(2)}) copy-start(bf16[1536]{0:T(1024)(128)(2,1)} %param.9) | copy-start | bytes 9220
  1.8 7.1 %collective-permute-start.2 = (bf16[12,128]{1,0:T(8,128)(2,1)S(1)}, bf16[12,128]{1,0:T(8,128)(2,1)S(1)}, u32[]{:S(2)}, u32[]{:S(2)}) collective-permute-start(bf16[12,128]{1,0:T(8,128)(2,1)S(1)} %get-tuple-element.11.mine), channel_id=1, source_target_pairs={{0,2},{1,3},{2,0},{3,1},{4,6},{5,7},{6,4},{7,5},{8,10},{9,11},{10,... | collective-permute-start | bytes 9224 | tf_op jit(solution)/shard_map/ppermute | solution.py:198
  5.7 3.7 %collective-permute-start.1 = (bf16[12,128]{1,0:T(8,128)(2,1)S(1)}, bf16[12,128]{1,0:T(8,128)(2,1)S(1)}, u32[]{:S(2)}, u32[]{:S(2)}) collective-permute-start(bf16[12,128]{1,0:T(8,128)(2,1)S(1)} %get-tuple-element.11.mine), channel_id=1, source_target_pairs={{0,1},{1,2},{2,3},{3,0},{4,5},{5,6},{6,7},{7,4},{8,9},{9,10},{10,1... | collective-permute-start | bytes 9224 | tf_op jit(solution)/shard_map/ppermute | solution.py:198
  6.1 3.3 %collective-permute-start = (bf16[12,128]{1,0:T(8,128)(2,1)S(1)}, bf16[12,128]{1,0:T(8,128)(2,1)S(1)}, u32[]{:S(2)}, u32[]{:S(2)}) collective-permute-start(bf16[12,128]{1,0:T(8,128)(2,1)S(1)} %get-tuple-element.11.mine), channel_id=1, source_target_pairs={{0,3},{1,0},{2,1},{3,2},{4,7},{5,4},{6,5},{7,6},{8,11},{9,8},{10,9... | collective-permute-start | bytes 9224 | tf_op jit(solution)/shard_map/ppermute | solution.py:198
  29.5 1.7 %collective-permute-start.3 = (bf16[32,48,128]{2,1,0:T(8,128)(2,1)S(1)}, bf16[32,48,128]{2,1,0:T(8,128)(2,1)S(1)}, u32[]{:S(2)}, u32[]{:S(2)}) collective-permute-start(bf16[32,48,128]{2,1,0:T(8,128)(2,1)S(1)} %all_to_all.5.recv), channel_id=1, source_target_pairs={{0,4},{4,0},{8,12},{12,8},{16,20},{20,16},{24,28},{28,24},{32,36},... | collective-permute-start | bytes 1179656 | tf_op jit(solution)/shard_map/ppermute | solution.py:209
  29.5 1.7 %copy-start = (f32[1536]{0:T(1024)S(1)}, f32[1536]{0:T(1024)}, u32[]{:S(2)}) copy-start(f32[1536]{0:T(1024)} %param.11) | copy-start | bytes 18436

commit v5 on v4

--- a/solution.py
+++ b/solution.py
@@ -77,14 +77,14 @@
     place = 0
     for s in range(sources):
         wide[s * each : s * each + each // 2, :] = cells[s, : each // 2, :].astype(jnp.float32)
-        wide[s * each + each // 2 : (s + 1) * each, :] = weights[s, each // 2 :, :].astype(jnp.float32)
+        wide[s * each + each // 2 : (s + 1) * each, :] = weights[s, weights.shape[1] - each // 2 :, :].astype(jnp.float32)
     for s in range(sources):
         for j, top in enumerate((first, first + half, 4 * half, 5 * half, 6 * half)):
             columns[j, pl.ds(place, half), :] = wide[s * each + top : s * each + top + half, :]
         used = wide[s * each + 7 * half : s * each + 7 * half + 1, :][0, 0].astype(jnp.int32)
         place = place + counts(used)
     for j in range(5):
-        columns[j, pl.ds(place, GROUP), :] = jnp.zeros((GROUP, LANES), jnp.float32)
+        columns[j, pl.ds(place, GROUP + 4), :] = jnp.zeros((GROUP + 4, LANES), jnp.float32)
     slots = lax.broadcasted_iota(jnp.int32, (2 * KIDS, LANES), 0).astype(jnp.float32).astype(jnp.bfloat16)
     levels = lax.broadcasted_iota(jnp.int32, (LANES, LANES), 0).astype(jnp.float32).astype(jnp.bfloat16)
     zero = jnp.zeros((), jnp.bfloat16)
@@ -93,34 +93,46 @@
     def spread(row, height):
         return jnp.broadcast_to(row, (height, LANES)).astype(jnp.bfloat16)
 
-    def block(at):
-        grad = spread(columns[2, pl.ds(at, 1), :], 2 * KIDS)
-        hess = spread(columns[3, pl.ds(at, 1), :], 2 * KIDS)
-        child = columns[4, pl.ds(at, 1), :]
-        upper = []
-        lower = []
-        for f in range(2):
-            cell = columns[f, pl.ds(at, 1), :]
-            high = cell >= LANES
-            low = spread(jnp.where(high, cell - LANES, cell), LANES)
-            slot = spread(jnp.where(high, child + KIDS, child), 2 * KIDS)
-            hit = slot == slots
-            upper += [jnp.where(hit, grad, zero), jnp.where(hit, hess, zero)]
-            lower.append(jnp.where(low == levels, one, zero))
-        return jnp.concatenate(upper, 0), jnp.concatenate(lower, 0)
+    def upper(at):
+        halves = []
+        for k in range(2):
+            grad = spread(columns[2, pl.ds(at + k, 1), :], 2 * KIDS)
+            hess = spread(columns[3, pl.ds(at + k, 1), :], 2 * KIDS)
+            child = columns[4, pl.ds(at + k, 1), :]
+            parts = []
+            for f in range(2):
+                slot = jnp.where(columns[f, pl.ds(at + k, 1), :] >= LANES, child + KIDS, child)
+                hit = spread(slot, 2 * KIDS) == slots
+                parts += [jnp.where(hit, grad, zero), jnp.where(hit, hess, zero)]
+            halves.append(jnp.concatenate(parts, 0))
+        return jnp.concatenate(halves, 1)
+
+    def lower(at):
+        halves = []
+        for k in range(2):
+            parts = []
+            for f in range(2):
+                cell = columns[f, pl.ds(at + k, 1), :]
+                low = spread(jnp.where(cell >= LANES, cell - LANES, cell), LANES)
+                parts.append(jnp.where(low == levels, one, zero))
+            halves.append(jnp.concatenate(parts, 0))
+        return jnp.concatenate(halves, 1).astype(LOW)
+
+    def push(chunk, base):
+        pltpu.matmul_push_rhs(lower(base + 2 * chunk), staging_register=(chunk // 2) % 2, mxu_index=chunk % 2, transpose=True)
 
     def step(i, carry):
         base = i * GROUP
-        for k in range(0, GROUP, 2):
-            first, second = block(base + k), block(base + k + 1)
-            upper = jnp.concatenate([first[0], second[0]], 1)
-            lower = jnp.concatenate([first[1], second[1]], 1).astype(LOW)
-            unit, slot = (k // 2) % 2, (k // 4) % 2
-            pltpu.matmul_push_rhs(lower, staging_register=slot, mxu_index=unit, transpose=True)
-            pltpu.matmul_acc_lhs(accs[unit], upper, load_staged_rhs=slot)
+        for chunk in range(GROUP // 2):
+            pltpu.matmul_acc_lhs(accs[chunk % 2], upper(base + 2 * chunk), load_staged_rhs=(chunk // 2) % 2)
+            push(chunk + 2, base)
         return carry
 
+    push(0, 0)
+    push(1, 0)
     lax.fori_loop(0, (place + GROUP - 1) // GROUP, step, 0)
+    for acc in accs:
+        pltpu.matmul_acc_lhs(acc, jnp.zeros((8 * KIDS, B), jnp.bfloat16), load_staged_rhs=0)
     return pltpu.matmul_pop(accs[0]) + pltpu.matmul_pop(accs[1])
 
 
@@ -178,7 +190,7 @@
     here = pl.BlockSpec(memory_space=pltpu.HBM)
     height = 2 * each
     wide = pltpu.VMEM((owners * height, LANES), jnp.float32)
-    columns = pltpu.VMEM((5, owners * blocks // 2 + GROUP, LANES), jnp.float32)
+    columns = pltpu.VMEM((5, owners * blocks // 2 + GROUP + 8, LANES), jnp.float32)
     part, packed = pl.pallas_call(
         split_kernel,
         out_shape=(shape((blocks, LANES), jnp.bfloat16), shape((owners, each, LANES), jnp.bfloat16)),
@@ -195,7 +207,7 @@
         name="split_rows",
         compiler_params=SMALL,
     )(*(pltpu.with_memory_space_constraint(x, pltpu.HBM) for x in (bins, tall(leaf), split_feature, split_bin)))
-    others = [lax.ppermute(part, "feat", [(i, (i + s) % feats) for i in range(feats)]) for s in (3, 1, 2)]
+    others = [lax.ppermute(part, "feat", [(i, (i + s) % feats) for i in range(feats)]) for s in (2, 1, 3)]
     send, code = pl.pallas_call(
         fill_kernel,
         out_shape=(shape((owners, height, LANES), jnp.bfloat16), shape((blocks, LANES), jnp.int32)),
@@ -206,7 +218,7 @@
         compiler_params=SMALL,
     )(row_counts, packed, tall(gradients), tall(hessians), part, *others)
     recv = lax.all_to_all(send, "rows", 0, 0, tiled=True)
-    other = lax.ppermute(recv, "rows", [(i, i ^ 1) for i in range(owners)])
+    other = lax.ppermute(recv[:, each:, :], "rows", [(i, i ^ 1) for i in range(owners)])
     partial = pl.pallas_call(
         first_kernel,
         out_shape=shape((2, 4 * KIDS, LANES), jnp.float32),

time: 33.6 us -> 33.4 us (level)
  Pallas kernels: 4.95 us -> 4.45 us
  transfers between devices with their start and end apart: 4 -> 4, of which waited for: 2 -> 2; matrix products, arithmetic and copies ran while one was open for 0% -> 0% of each run, Pallas kernels for 5% -> 4%
where the time goes in v5:
time: 33.4 us; the launch traced here: 33.1 us
  blocking collectives  20.1 us (60%)
  starting transfers between devices  6.57 us (20%)
  Pallas kernels  4.45 us (13%)
  between operations  1.36 us (4%)
  waiting for transfers between devices  0.55 us (2%)
    all_to_all x1, blocking collectives, body(): recv = lax.all_to_all(send, 'rows', 0, 0, tiled=True)  20.1 us
    ppermute x3, starting transfers between devices, body(): lax.ppermute(part, 'feat', [(i, (i + s) % feats) for i in range(feats)])  6.49 us
    pallas_call x1, Pallas kernels, body(): pl.pallas_call(last_kernel, out_shape=(shape((2, 2, KIDS, B), jnp.float32...  2.03 us
    pallas_call x1, Pallas kernels, body(): pl.pallas_call(first_kernel, out_shape=shape((2, 4 * KIDS, LANES), jnp.fl...  1.19 us
    pallas_call x1, Pallas kernels, body(): pl.pallas_call(split_kernel, out_shape=(shape((blocks, LANES), jnp.bfloat...  1.18 us
  transfers between devices with their start and end apart: 4, of which 2 were waited for; matrix products, arithmetic and copies ran while one was open for 0% of the time, Pallas kernels for 4%

profile of v5, /device:TPU:1, one launch (start us, length us, event | category | flops | bytes accessed | tf_op | source)
XLA Modules:
  0.0 33.1 jit_solution(10686123255382160618)
XLA Ops:
  0.6 1.2 %split_rows.1 = (bf16[12,128]{1,0:T(8,128)(2,1)S(1)}, bf16[32,24,128]{2,1,0:T(8,128)(2,1)S(1)}) custom-call(s32[64,1536]{1,0:T(8,128)} %bins.1, s32[12,128]{1,0:T(8,128)} %bitcast.10, s32[8]{0:T(128)} %features.1, s32[8]{0:T(128)} %cutoffs.1), custom_call_target="tpu_custom_call" | custom-call | tf_op jit(solution)/shard_map/split_rows/pallas_call | solution.py:194
  1.8 0.0 copy-start.2
  1.8 0.0 copy-start.1
  1.8 3.8 %collective-permute-start = (bf16[12,128]{1,0:T(8,128)(2,1)S(1)}, bf16[12,128]{1,0:T(8,128)(2,1)S(1)}, u32[]{:S(2)}, u32[]{:S(2)}) collective-permute-start(bf16[12,128]{1,0:T(8,128)(2,1)S(1)} %get-tuple-element.11.mine), channel_id=1, source_target_pairs={{0,2},{1,3},{2,0},{3,1},{4,6},{5,7},{6,4},{7,5},{8,10},{9,11},{10,... | collective-permute-start | bytes 9224 | tf_op jit(solution)/shard_map/ppermute | solution.py:210
  5.7 0.4 %collective-permute-start.1 = (bf16[12,128]{1,0:T(8,128)(2,1)S(1)}, bf16[12,128]{1,0:T(8,128)(2,1)S(1)}, u32[]{:S(2)}, u32[]{:S(2)}) collective-permute-start(bf16[12,128]{1,0:T(8,128)(2,1)S(1)} %get-tuple-element.11.mine), channel_id=1, source_target_pairs={{0,1},{1,2},{2,3},{3,0},{4,5},{5,6},{6,7},{7,4},{8,9},{9,10},{10,1... | collective-permute-start | bytes 9224 | tf_op jit(solution)/shard_map/ppermute | solution.py:210
  6.1 2.3 %collective-permute-start.2 = (bf16[12,128]{1,0:T(8,128)(2,1)S(1)}, bf16[12,128]{1,0:T(8,128)(2,1)S(1)}, u32[]{:S(2)}, u32[]{:S(2)}) collective-permute-start(bf16[12,128]{1,0:T(8,128)(2,1)S(1)} %get-tuple-element.11.mine), channel_id=1, source_target_pairs={{0,3},{1,0},{2,1},{3,2},{4,7},{5,4},{6,5},{7,6},{8,11},{9,8},{10,9... | collective-permute-start | bytes 9224 | tf_op jit(solution)/shard_map/ppermute | solution.py:210
  9.0 0.0 collective-permute-done.one
  9.0 0.3 collective-permute-done.1.two
  9.3 0.0 collective-permute-done.2.three
  9.3 0.0 copy-done.2
  9.3 0.0 copy-done.1
  9.4 20.1 %all_to_all.5.recv = bf16[32,48,128]{2,1,0:T(8,128)(2,1)S(1)} all-to-all(bf16[32,48,128]{2,1,0:T(8,128)(2,1)S(1)} %get-tuple-element.12), channel_id=1, replica_groups=mesh['rows'=32,'feat'=4] {'rows'}, dimensions={0} | all-to-all | bytes 786432 | tf_op jit(solution)/shard_map/all_to_all | solution.py:220
  29.5 0.1 collective-permute-start.3
  29.6 0.0 copy-start
  29.6 1.2 %first_half.1.partial = f32[2,64,128]{2,1,0:T(8,128)S(1)} custom-call(bf16[32,48,128]{2,1,0:T(8,128)(2,1)S(1)} %all_to_all.5.recv), custom_call_target="tpu_custom_call" | custom-call | flops 1073741824 | bytes 1048576 | tf_op jit(solution)/shard_map/first_half/pallas_call | solution.py:222
  30.8 0.2 collective-permute-done.3.other
  31.0 0.0 copy-done
  31.0 2.0 %histograms.1 = (f32[2,2,16,256]{3,2,1,0:T(8,128)}, s32[12,128]{1,0:T(8,128)}, f32[12,128]{1,0:T(8,128)}) custom-call(bf16[32,48,128]{2,1,0:T(8,128)(2,1)S(1)} %all_to_all.5.recv, bf16[32,24,128]{2,1,0:T(8,128)(2,1)S(1)} %collective-permute-done.3.other, f32[2,64,128]{2,1,0:T(8,128)S(1)} %first_half.1.partial, s32[12,128]{1,0:T(8,128)S(1)} %get-tuple-element.13.code, ...), custom_call_target="tpu_custom_call" | custom-call | tf_op jit(solution)/shard_map/histograms/pallas_call | solution.py:232
  (2 shorter events, 0.1 us)
Async XLA Ops:
  1.8 7.5 %copy-start.2 = (bf16[1536]{0:T(1024)(128)(2,1)S(1)}, bf16[1536]{0:T(1024)(128)(2,1)}, u32[]{:S(2)}) copy-start(bf16[1536]{0:T(1024)(128)(2,1)} %param.10) | copy-start | bytes 9220
  1.8 7.5 %copy-start.1 = (bf16[1536]{0:T(1024)(128)(2,1)S(1)}, bf16[1536]{0:T(1024)(128)(2,1)}, u32[]{:S(2)}) copy-start(bf16[1536]{0:T(1024)(128)(2,1)} %param.9) | copy-start | bytes 9220
  1.8 7.1 %collective-permute-start = (bf16[12,128]{1,0:T(8,128)(2,1)S(1)}, bf16[12,128]{1,0:T(8,128)(2,1)S(1)}, u32[]{:S(2)}, u32[]{:S(2)}) collective-permute-start(bf16[12,128]{1,0:T(8,128)(2,1)S(1)} %get-tuple-element.11.mine), channel_id=1, source_target_pairs={{0,2},{1,3},{2,0},{3,1},{4,6},{5,7},{6,4},{7,5},{8,10},{9,11},{10,... | collective-permute-start | bytes 9224 | tf_op jit(solution)/shard_map/ppermute | solution.py:210
  5.7 3.7 %collective-permute-start.1 = (bf16[12,128]{1,0:T(8,128)(2,1)S(1)}, bf16[12,128]{1,0:T(8,128)(2,1)S(1)}, u32[]{:S(2)}, u32[]{:S(2)}) collective-permute-start(bf16[12,128]{1,0:T(8,128)(2,1)S(1)} %get-tuple-element.11.mine), channel_id=1, source_target_pairs={{0,1},{1,2},{2,3},{3,0},{4,5},{5,6},{6,7},{7,4},{8,9},{9,10},{10,1... | collective-permute-start | bytes 9224 | tf_op jit(solution)/shard_map/ppermute | solution.py:210
  6.1 3.3 %collective-permute-start.2 = (bf16[12,128]{1,0:T(8,128)(2,1)S(1)}, bf16[12,128]{1,0:T(8,128)(2,1)S(1)}, u32[]{:S(2)}, u32[]{:S(2)}) collective-permute-start(bf16[12,128]{1,0:T(8,128)(2,1)S(1)} %get-tuple-element.11.mine), channel_id=1, source_target_pairs={{0,3},{1,0},{2,1},{3,2},{4,7},{5,4},{6,5},{7,6},{8,11},{9,8},{10,9... | collective-permute-start | bytes 9224 | tf_op jit(solution)/shard_map/ppermute | solution.py:210
  29.5 1.5 %collective-permute-start.3 = (bf16[32,24,128]{2,1,0:T(8,128)(2,1)S(1)}, bf16[32,24,128]{2,1,0:T(8,128)(2,1)S(1)}, u32[]{:S(2)}, u32[]{:S(2)}) collective-permute-start(bf16[32,24,128]{2,1,0:T(8,128)(2,1)S(1)} %slice.4), channel_id=1, source_target_pairs={{0,4},{4,0},{8,12},{12,8},{16,20},{20,16},{24,28},{28,24},{32,36},... | collective-permute-start | bytes 589832 | tf_op jit(solution)/shard_map/ppermute | solution.py:221
  29.6 1.4 %copy-start = (f32[1536]{0:T(1024)S(1)}, f32[1536]{0:T(1024)}, u32[]{:S(2)}) copy-start(f32[1536]{0:T(1024)} %param.11) | copy-start | bytes 18436

commit v6 on v5

--- a/solution.py
+++ b/solution.py
@@ -59,7 +59,7 @@
     stage[0:blocks, :] = jnp.where(live, gradients[...].astype(jnp.float32), 0.0)
     stage[blocks : 2 * blocks, :] = jnp.where(live, hessians[...].astype(jnp.float32), 0.0)
     stage[2 * blocks : 3 * blocks, :] = total
-    stage[3 * blocks :, :] = jnp.full((blocks, LANES), used, jnp.int32).astype(jnp.float32)
+    stage[3 * blocks : 4 * blocks, :] = jnp.full((blocks, LANES), used, jnp.int32).astype(jnp.float32)
     tails = []
     for core in range(2):
         rows = [stage[pl.ds(j * blocks + core, half, stride=2), :] for j in range(4)]
@@ -189,8 +189,8 @@
     tall = lambda x: x.reshape(blocks, LANES)
     here = pl.BlockSpec(memory_space=pltpu.HBM)
     height = 2 * each
-    wide = pltpu.VMEM((owners * height, LANES), jnp.float32)
-    columns = pltpu.VMEM((5, owners * blocks // 2 + GROUP + 8, LANES), jnp.float32)
+    wide = pltpu.VMEM((owners * height + 8, LANES), jnp.float32)
+    columns = pltpu.VMEM((5, owners * blocks // 2 + GROUP + 16, LANES), jnp.float32)
     part, packed = pl.pallas_call(
         split_kernel,
         out_shape=(shape((blocks, LANES), jnp.bfloat16), shape((owners, each, LANES), jnp.bfloat16)),
@@ -198,7 +198,7 @@
         out_specs=(VMEM, VMEM),
         scratch_shapes=[
             pltpu.VMEM((width, length), jnp.int32),
-            pltpu.VMEM((width * blocks, LANES), jnp.int32),
+            pltpu.VMEM((width * blocks + 8, LANES), jnp.int32),
             pltpu.VMEM((blocks, LANES), jnp.int32),
             pltpu.SMEM((LEAVES,), jnp.int32),
             pltpu.SMEM((LEAVES,), jnp.int32),
@@ -213,7 +213,7 @@
         out_shape=(shape((owners, height, LANES), jnp.bfloat16), shape((blocks, LANES), jnp.int32)),
         in_specs=[SMEM] + [VMEM] * 7,
         out_specs=(VMEM, VMEM),
-        scratch_shapes=[pltpu.VMEM((4 * blocks, LANES), jnp.float32)],
+        scratch_shapes=[pltpu.VMEM((4 * blocks + 8, LANES), jnp.float32)],
         name="fill_messages",
         compiler_params=SMALL,
     )(row_counts, packed, tall(gradients), tall(hessians), part, *others)

time: 33.4 us -> 33.3 us (level)
  no operation moved by 1% of the time
where the time goes in v6:
time: 33.3 us; the launch traced here: 33.1 us
  blocking collectives  20.1 us (60%)
  starting transfers between devices  6.57 us (20%)
  Pallas kernels  4.49 us (13%)
  between operations  1.36 us (4%)
  waiting for transfers between devices  0.54 us (2%)
    all_to_all x1, blocking collectives, body(): recv = lax.all_to_all(send, 'rows', 0, 0, tiled=True)  20.1 us
    ppermute x3, starting transfers between devices, body(): lax.ppermute(part, 'feat', [(i, (i + s) % feats) for i in range(feats)])  6.49 us
    pallas_call x1, Pallas kernels, body(): pl.pallas_call(last_kernel, out_shape=(shape((2, 2, KIDS, B), jnp.float32...  2.06 us
    pallas_call x1, Pallas kernels, body(): pl.pallas_call(first_kernel, out_shape=shape((2, 4 * KIDS, LANES), jnp.fl...  1.2 us
    pallas_call x1, Pallas kernels, body(): pl.pallas_call(split_kernel, out_shape=(shape((blocks, LANES), jnp.bfloat...  1.18 us
  transfers between devices with their start and end apart: 4, of which 2 were waited for; matrix products, arithmetic and copies ran while one was open for 0% of the time, Pallas kernels for 4%

profile of v6, /device:TPU:1, one launch (start us, length us, event | category | flops | bytes accessed | tf_op | source)
XLA Modules:
  0.0 33.1 jit_solution(3803145805508586059)
XLA Ops:
  0.6 1.2 %split_rows.1 = (bf16[12,128]{1,0:T(8,128)(2,1)S(1)}, bf16[32,24,128]{2,1,0:T(8,128)(2,1)S(1)}) custom-call(s32[64,1536]{1,0:T(8,128)} %bins.1, s32[12,128]{1,0:T(8,128)} %bitcast.10, s32[8]{0:T(128)} %features.1, s32[8]{0:T(128)} %cutoffs.1), custom_call_target="tpu_custom_call" | custom-call | tf_op jit(solution)/shard_map/split_rows/pallas_call | solution.py:194
  1.8 0.0 copy-start.2
  1.8 0.0 copy-start.1
  1.8 3.8 %collective-permute-start = (bf16[12,128]{1,0:T(8,128)(2,1)S(1)}, bf16[12,128]{1,0:T(8,128)(2,1)S(1)}, u32[]{:S(2)}, u32[]{:S(2)}) collective-permute-start(bf16[12,128]{1,0:T(8,128)(2,1)S(1)} %get-tuple-element.11.mine), channel_id=1, source_target_pairs={{0,2},{1,3},{2,0},{3,1},{4,6},{5,7},{6,4},{7,5},{8,10},{9,11},{10,... | collective-permute-start | bytes 9224 | tf_op jit(solution)/shard_map/ppermute | solution.py:210
  5.7 0.4 %collective-permute-start.1 = (bf16[12,128]{1,0:T(8,128)(2,1)S(1)}, bf16[12,128]{1,0:T(8,128)(2,1)S(1)}, u32[]{:S(2)}, u32[]{:S(2)}) collective-permute-start(bf16[12,128]{1,0:T(8,128)(2,1)S(1)} %get-tuple-element.11.mine), channel_id=1, source_target_pairs={{0,1},{1,2},{2,3},{3,0},{4,5},{5,6},{6,7},{7,4},{8,9},{9,10},{10,1... | collective-permute-start | bytes 9224 | tf_op jit(solution)/shard_map/ppermute | solution.py:210
  6.1 2.3 %collective-permute-start.2 = (bf16[12,128]{1,0:T(8,128)(2,1)S(1)}, bf16[12,128]{1,0:T(8,128)(2,1)S(1)}, u32[]{:S(2)}, u32[]{:S(2)}) collective-permute-start(bf16[12,128]{1,0:T(8,128)(2,1)S(1)} %get-tuple-element.11.mine), channel_id=1, source_target_pairs={{0,3},{1,0},{2,1},{3,2},{4,7},{5,4},{6,5},{7,6},{8,11},{9,8},{10,9... | collective-permute-start | bytes 9224 | tf_op jit(solution)/shard_map/ppermute | solution.py:210
  9.0 0.0 collective-permute-done.one
  9.0 0.3 collective-permute-done.1.two
  9.3 0.0 collective-permute-done.2.three
  9.3 0.0 copy-done.2
  9.3 0.0 copy-done.1
  9.4 20.1 %all_to_all.5.recv = bf16[32,48,128]{2,1,0:T(8,128)(2,1)S(1)} all-to-all(bf16[32,48,128]{2,1,0:T(8,128)(2,1)S(1)} %get-tuple-element.12), channel_id=1, replica_groups=mesh['rows'=32,'feat'=4] {'rows'}, dimensions={0} | all-to-all | bytes 786432 | tf_op jit(solution)/shard_map/all_to_all | solution.py:220
  29.5 0.1 collective-permute-start.3
  29.6 0.0 copy-start
  29.6 1.2 %first_half.1.partial = f32[2,64,128]{2,1,0:T(8,128)S(1)} custom-call(bf16[32,48,128]{2,1,0:T(8,128)(2,1)S(1)} %all_to_all.5.recv), custom_call_target="tpu_custom_call" | custom-call | flops 1073741824 | bytes 1048576 | tf_op jit(solution)/shard_map/first_half/pallas_call | solution.py:222
  30.8 0.2 collective-permute-done.3.other
  31.0 0.0 copy-done
  31.0 2.1 %histograms.1 = (f32[2,2,16,256]{3,2,1,0:T(8,128)}, s32[12,128]{1,0:T(8,128)}, f32[12,128]{1,0:T(8,128)}) custom-call(bf16[32,48,128]{2,1,0:T(8,128)(2,1)S(1)} %all_to_all.5.recv, bf16[32,24,128]{2,1,0:T(8,128)(2,1)S(1)} %collective-permute-done.3.other, f32[2,64,128]{2,1,0:T(8,128)S(1)} %first_half.1.partial, s32[12,128]{1,0:T(8,128)S(1)} %get-tuple-element.13.code, ...), custom_call_target="tpu_custom_call" | custom-call | tf_op jit(solution)/shard_map/histograms/pallas_call | solution.py:232
  (2 shorter events, 0.1 us)
Async XLA Ops:
  1.8 7.5 %copy-start.2 = (bf16[1536]{0:T(1024)(128)(2,1)S(1)}, bf16[1536]{0:T(1024)(128)(2,1)}, u32[]{:S(2)}) copy-start(bf16[1536]{0:T(1024)(128)(2,1)} %param.10) | copy-start | bytes 9220
  1.8 7.5 %copy-start.1 = (bf16[1536]{0:T(1024)(128)(2,1)S(1)}, bf16[1536]{0:T(1024)(128)(2,1)}, u32[]{:S(2)}) copy-start(bf16[1536]{0:T(1024)(128)(2,1)} %param.9) | copy-start | bytes 9220
  1.8 7.1 %collective-permute-start = (bf16[12,128]{1,0:T(8,128)(2,1)S(1)}, bf16[12,128]{1,0:T(8,128)(2,1)S(1)}, u32[]{:S(2)}, u32[]{:S(2)}) collective-permute-start(bf16[12,128]{1,0:T(8,128)(2,1)S(1)} %get-tuple-element.11.mine), channel_id=1, source_target_pairs={{0,2},{1,3},{2,0},{3,1},{4,6},{5,7},{6,4},{7,5},{8,10},{9,11},{10,... | collective-permute-start | bytes 9224 | tf_op jit(solution)/shard_map/ppermute | solution.py:210
  5.7 3.7 %collective-permute-start.1 = (bf16[12,128]{1,0:T(8,128)(2,1)S(1)}, bf16[12,128]{1,0:T(8,128)(2,1)S(1)}, u32[]{:S(2)}, u32[]{:S(2)}) collective-permute-start(bf16[12,128]{1,0:T(8,128)(2,1)S(1)} %get-tuple-element.11.mine), channel_id=1, source_target_pairs={{0,1},{1,2},{2,3},{3,0},{4,5},{5,6},{6,7},{7,4},{8,9},{9,10},{10,1... | collective-permute-start | bytes 9224 | tf_op jit(solution)/shard_map/ppermute | solution.py:210
  6.1 3.3 %collective-permute-start.2 = (bf16[12,128]{1,0:T(8,128)(2,1)S(1)}, bf16[12,128]{1,0:T(8,128)(2,1)S(1)}, u32[]{:S(2)}, u32[]{:S(2)}) collective-permute-start(bf16[12,128]{1,0:T(8,128)(2,1)S(1)} %get-tuple-element.11.mine), channel_id=1, source_target_pairs={{0,3},{1,0},{2,1},{3,2},{4,7},{5,4},{6,5},{7,6},{8,11},{9,8},{10,9... | collective-permute-start | bytes 9224 | tf_op jit(solution)/shard_map/ppermute | solution.py:210
  29.5 1.5 %collective-permute-start.3 = (bf16[32,24,128]{2,1,0:T(8,128)(2,1)S(1)}, bf16[32,24,128]{2,1,0:T(8,128)(2,1)S(1)}, u32[]{:S(2)}, u32[]{:S(2)}) collective-permute-start(bf16[32,24,128]{2,1,0:T(8,128)(2,1)S(1)} %slice.4), channel_id=1, source_target_pairs={{0,4},{4,0},{8,12},{12,8},{16,20},{20,16},{24,28},{28,24},{32,36},... | collective-permute-start | bytes 589832 | tf_op jit(solution)/shard_map/ppermute | solution.py:221
  29.6 1.4 %copy-start = (f32[1536]{0:T(1024)S(1)}, f32[1536]{0:T(1024)}, u32[]{:S(2)}) copy-start(f32[1536]{0:T(1024)} %param.11) | copy-start | bytes 18436

commit v7 on v6

--- a/solution.py
+++ b/solution.py
@@ -10,6 +10,7 @@
 KIDS = 2 * LEAVES
 LANES = 128
 GROUP = 16
+DEAD = 64.0
 LOW = jnp.float8_e4m3fn
 VMEM = pl.BlockSpec(memory_space=pltpu.VMEM)
 SMALL = pltpu.CompilerParams(vmem_limit_bytes=16 << 20)
@@ -39,50 +40,49 @@
         code = jnp.where(leaves[...] == slot, child, code)
     part[...] = code.astype(jnp.float32).astype(jnp.bfloat16)
     owners, each, _ = packed.shape
-    half = blocks // 2
     for owner in range(owners):
-        order = [(parity, top) for parity in (owner % 2, 1 - owner % 2) for top in range(owner * each, (owner + 1) * each, blocks)]
-        picked = [rows[pl.ds(top + parity, half, stride=2), :].astype(jnp.float32) for parity, top in order]
+        core = owner % 2
+        order = [(start, top) for start in (2 * core, 1, 2 - 2 * core) for top in range(owner * each, (owner + 1) * each, blocks)]
+        picked = [rows[pl.ds(top + start, blocks // 3, stride=3), :].astype(jnp.float32) for start, top in order]
         packed[owner] = jnp.concatenate(picked, 0).astype(jnp.bfloat16)
 
 
 def fill_kernel(count, packed, gradients, hessians, mine, one, two, three, send, code, stage):
     owners, each, _ = packed.shape
     blocks = mine.shape[0]
-    half = blocks // 2
     total = sum(x[...].astype(jnp.float32) for x in (mine, one, two, three))
     code[...] = total.astype(jnp.int32)
     spot = lax.broadcasted_iota(jnp.int32, (blocks, LANES), 0) * LANES
     spot = spot + lax.broadcasted_iota(jnp.int32, (blocks, LANES), 1)
     live = spot < count[0]
-    used = (count[0] + LANES - 1) // LANES
-    stage[0:blocks, :] = jnp.where(live, gradients[...].astype(jnp.float32), 0.0)
-    stage[blocks : 2 * blocks, :] = jnp.where(live, hessians[...].astype(jnp.float32), 0.0)
-    stage[2 * blocks : 3 * blocks, :] = total
-    stage[3 * blocks : 4 * blocks, :] = jnp.full((blocks, LANES), used, jnp.int32).astype(jnp.float32)
+    stage[0:blocks, :] = gradients[...].astype(jnp.float32)
+    stage[blocks : 2 * blocks, :] = hessians[...].astype(jnp.float32)
+    stage[2 * blocks : 3 * blocks, :] = jnp.where(live, total, DEAD)
     tails = []
     for core in range(2):
-        rows = [stage[pl.ds(j * blocks + core, half, stride=2), :] for j in range(4)]
+        rows = [stage[pl.ds(j * blocks + start, blocks // 3, stride=3), :] for start in (2 * core, 1) for j in range(3)]
         tails.append(jnp.concatenate(rows, 0).astype(jnp.bfloat16))
     for owner in range(owners):
         send[owner, 0:each, :] = packed[owner]
         send[owner, each:, :] = tails[owner % 2]
 
 
-def accumulate(cells, first, weights, counts, wide, columns, accs):
-    sources, each, _ = cells.shape
-    half = each // 8
+def accumulate(lists, size, sources, each, wide, tally, columns, accs):
     for acc in accs:
         pltpu.matmul_pop(acc)
+    for n, tops in enumerate(lists):
+        alive = jnp.zeros((sources, LANES), jnp.float32)
+        for k in range(size):
+            kids = wide[pl.ds(tops[4] + k, sources, stride=each), :]
+            alive += jnp.where(kids < DEAD, 1.0, 0.0)
+        tally[n * sources : (n + 1) * sources, :] = alive
     place = 0
     for s in range(sources):
-        wide[s * each : s * each + each // 2, :] = cells[s, : each // 2, :].astype(jnp.float32)
-        wide[s * each + each // 2 : (s + 1) * each, :] = weights[s, weights.shape[1] - each // 2 :, :].astype(jnp.float32)
-    for s in range(sources):
-        for j, top in enumerate((first, first + half, 4 * half, 5 * half, 6 * half)):
-            columns[j, pl.ds(place, half), :] = wide[s * each + top : s * each + top + half, :]
-        used = wide[s * each + 7 * half : s * each + 7 * half + 1, :][0, 0].astype(jnp.int32)
-        place = place + counts(used)
+        for n, tops in enumerate(lists):
+            for j, top in enumerate(tops):
+                columns[j, pl.ds(place, size), :] = wide[s * each + top : s * each + top + size, :]
+            row = n * sources + s
+            place = place + tally[row : row + 1, :][0, 0].astype(jnp.int32)
     for j in range(5):
         columns[j, pl.ds(place, GROUP + 4), :] = jnp.zeros((GROUP + 4, LANES), jnp.float32)
     slots = lax.broadcasted_iota(jnp.int32, (2 * KIDS, LANES), 0).astype(jnp.float32).astype(jnp.bfloat16)
@@ -144,22 +144,32 @@
     )
 
 
-def first_kernel(recv, partial, wide, columns):
-    core = lax.rem(lax.axis_index("rows"), 2)
+def first_kernel(recv, partial, wide, tally, columns):
+    sources, each, _ = recv.shape
+    size = each // 12
 
     def steps(accs):
-        total = accumulate(recv, 0, recv, lambda used: (used + 1 - core) >> 1, wide, columns, accs)
+        for s in range(sources):
+            wide[s * each : (s + 1) * each, :] = recv[s].astype(jnp.float32)
+        lists = [tuple(size * k for k in (0, 1, 6, 7, 8)), tuple(size * k for k in (2, 3, 9, 10, 11))]
+        total = accumulate(lists, size, sources, each, wide, tally, columns, accs)
         for f in range(2):
             partial[f] = total[f * 4 * KIDS : (f + 1) * 4 * KIDS, f * LANES : (f + 1) * LANES]
 
     scoped(steps)
 
 
-def last_kernel(recv, other, partial, code, predictions, hist, new_leaf, new_pred, wide, columns):
-    core = lax.rem(lax.axis_index("rows"), 2)
+def last_kernel(recv, other, partial, code, predictions, hist, new_leaf, new_pred, wide, tally, columns):
+    sources, each, _ = recv.shape
+    size = each // 12
 
     def steps(accs):
-        total = accumulate(recv, recv.shape[1] // 4, other, lambda used: (used + core) >> 1, wide, columns, accs)
+        for s in range(sources):
+            top = s * 6 * size
+            wide[top : top + 2 * size, :] = recv[s, 4 * size : 6 * size, :].astype(jnp.float32)
+            wide[top + 2 * size : top + 5 * size, :] = other[s].astype(jnp.float32)
+        lists = [tuple(size * k for k in (0, 1, 2, 3, 4))]
+        total = accumulate(lists, size, sources, 6 * size, wide, tally, columns, accs)
         for f in range(2):
             mine = partial[f] + total[f * 4 * KIDS : (f + 1) * 4 * KIDS, f * LANES : (f + 1) * LANES]
             for kind in range(2):
@@ -189,8 +199,8 @@
     tall = lambda x: x.reshape(blocks, LANES)
     here = pl.BlockSpec(memory_space=pltpu.HBM)
     height = 2 * each
-    wide = pltpu.VMEM((owners * height + 8, LANES), jnp.float32)
-    columns = pltpu.VMEM((5, owners * blocks // 2 + GROUP + 16, LANES), jnp.float32)
+    tally = pltpu.VMEM((2 * owners, LANES), jnp.float32)
+    columns = pltpu.VMEM((5, owners * blocks * 2 // 3 + GROUP + 16, LANES), jnp.float32)
     part, packed = pl.pallas_call(
         split_kernel,
         out_shape=(shape((blocks, LANES), jnp.bfloat16), shape((owners, each, LANES), jnp.bfloat16)),
@@ -207,7 +217,7 @@
         name="split_rows",
         compiler_params=SMALL,
     )(*(pltpu.with_memory_space_constraint(x, pltpu.HBM) for x in (bins, tall(leaf), split_feature, split_bin)))
-    others = [lax.ppermute(part, "feat", [(i, (i + s) % feats) for i in range(feats)]) for s in (2, 1, 3)]
+    others = [lax.ppermute(part, "feat", [(i, (i + s) % feats) for i in range(feats)]) for s in (3, 1, 2)]
     send, code = pl.pallas_call(
         fill_kernel,
         out_shape=(shape((owners, height, LANES), jnp.bfloat16), shape((blocks, LANES), jnp.int32)),
@@ -218,13 +228,13 @@
         compiler_params=SMALL,
     )(row_counts, packed, tall(gradients), tall(hessians), part, *others)
     recv = lax.all_to_all(send, "rows", 0, 0, tiled=True)
-    other = lax.ppermute(recv[:, each:, :], "rows", [(i, i ^ 1) for i in range(owners)])
+    other = lax.ppermute(recv[:, each : each + blocks, :], "rows", [(i, i ^ 1) for i in range(owners)])
     partial = pl.pallas_call(
         first_kernel,
         out_shape=shape((2, 4 * KIDS, LANES), jnp.float32),
         in_specs=[VMEM],
         out_specs=VMEM,
-        scratch_shapes=[wide, columns],
+        scratch_shapes=[pltpu.VMEM((owners * height + 8, LANES), jnp.float32), tally, columns],
         name="first_half",
         cost_estimate=pl.CostEstimate(flops=1 << 30, transcendentals=0, bytes_accessed=1 << 20),
         compiler_params=SMALL,
@@ -234,7 +244,7 @@
         out_shape=(shape((2, 2, KIDS, B), jnp.float32), shape((blocks, LANES), jnp.int32), shape((blocks, LANES), jnp.float32)),
         in_specs=[VMEM] * 5,
         out_specs=(VMEM, VMEM, VMEM),
-        scratch_shapes=[wide, columns],
+        scratch_shapes=[pltpu.VMEM((owners * each + 8, LANES), jnp.float32), tally, columns],
         name="histograms",
         compiler_params=SMALL,
     )(recv, other, partial, code, tall(predictions))

time: 33.3 us -> 33.4 us (level)
    pallas_call x1, Pallas kernels: 1.2 us -> 1.67 us  [body(): pl.pallas_call(first_kernel, out_shape=shape((2, 4 * KIDS, LANES), jnp.fl...]
  transfers between devices with their start and end apart: 4 -> 4, of which waited for: 2 -> 1; matrix products, arithmetic and copies ran while one was open for 0% -> 0% of each run, Pallas kernels for 4% -> 5%
where the time goes in v7:
time: 33.4 us; the launch traced here: 33.2 us
  blocking collectives  20.1 us (60%)
  starting transfers between devices  6.57 us (20%)
  Pallas kernels  4.79 us (14%)
  between operations  1.37 us (4%)
  waiting for transfers between devices  0.34 us (1%)
    all_to_all x1, blocking collectives, body(): recv = lax.all_to_all(send, 'rows', 0, 0, tiled=True)  20.1 us
    ppermute x3, starting transfers between devices, body(): lax.ppermute(part, 'feat', [(i, (i + s) % feats) for i in range(feats)])  6.49 us
    pallas_call x1, Pallas kernels, body(): pl.pallas_call(last_kernel, out_shape=(shape((2, 2, KIDS, B), jnp.float32...  1.88 us
    pallas_call x1, Pallas kernels, body(): pl.pallas_call(first_kernel, out_shape=shape((2, 4 * KIDS, LANES), jnp.fl...  1.67 us
    pallas_call x1, Pallas kernels, body(): pl.pallas_call(split_kernel, out_shape=(shape((blocks, LANES), jnp.bfloat...  1.2 us
  transfers between devices with their start and end apart: 4, of which 1 were waited for; matrix products, arithmetic and copies ran while one was open for 0% of the time, Pallas kernels for 5%

profile of v7, /device:TPU:1, one launch (start us, length us, event | category | flops | bytes accessed | tf_op | source)
XLA Modules:
  0.0 33.2 jit_solution(13614493819102690171)
XLA Ops:
  0.6 1.2 %split_rows.1 = (bf16[12,128]{1,0:T(8,128)(2,1)S(1)}, bf16[32,24,128]{2,1,0:T(8,128)(2,1)S(1)}) custom-call(s32[64,1536]{1,0:T(8,128)} %bins.1, s32[12,128]{1,0:T(8,128)} %bitcast.10, s32[8]{0:T(128)} %features.1, s32[8]{0:T(128)} %cutoffs.1), custom_call_target="tpu_custom_call" | custom-call | tf_op jit(solution)/shard_map/split_rows/pallas_call | solution.py:204
  1.8 0.0 copy-start.2
  1.9 0.0 copy-start.1
  1.9 3.8 %collective-permute-start.2 = (bf16[12,128]{1,0:T(8,128)(2,1)S(1)}, bf16[12,128]{1,0:T(8,128)(2,1)S(1)}, u32[]{:S(2)}, u32[]{:S(2)}) collective-permute-start(bf16[12,128]{1,0:T(8,128)(2,1)S(1)} %get-tuple-element.11.mine), channel_id=1, source_target_pairs={{0,2},{1,3},{2,0},{3,1},{4,6},{5,7},{6,4},{7,5},{8,10},{9,11},{10,... | collective-permute-start | bytes 9224 | tf_op jit(solution)/shard_map/ppermute | solution.py:220
  5.7 0.4 %collective-permute-start.1 = (bf16[12,128]{1,0:T(8,128)(2,1)S(1)}, bf16[12,128]{1,0:T(8,128)(2,1)S(1)}, u32[]{:S(2)}, u32[]{:S(2)}) collective-permute-start(bf16[12,128]{1,0:T(8,128)(2,1)S(1)} %get-tuple-element.11.mine), channel_id=1, source_target_pairs={{0,1},{1,2},{2,3},{3,0},{4,5},{5,6},{6,7},{7,4},{8,9},{9,10},{10,1... | collective-permute-start | bytes 9224 | tf_op jit(solution)/shard_map/ppermute | solution.py:220
  6.1 2.3 %collective-permute-start = (bf16[12,128]{1,0:T(8,128)(2,1)S(1)}, bf16[12,128]{1,0:T(8,128)(2,1)S(1)}, u32[]{:S(2)}, u32[]{:S(2)}) collective-permute-start(bf16[12,128]{1,0:T(8,128)(2,1)S(1)} %get-tuple-element.11.mine), channel_id=1, source_target_pairs={{0,3},{1,0},{2,1},{3,2},{4,7},{5,4},{6,5},{7,6},{8,11},{9,8},{10,9... | collective-permute-start | bytes 9224 | tf_op jit(solution)/shard_map/ppermute | solution.py:220
  9.0 0.0 collective-permute-done.2.three
  9.0 0.3 collective-permute-done.1.two
  9.3 0.0 collective-permute-done.one
  9.3 0.0 copy-done.2
  9.4 0.0 copy-done.1
  9.4 20.1 %all_to_all.5.recv = bf16[32,48,128]{2,1,0:T(8,128)(2,1)S(1)} all-to-all(bf16[32,48,128]{2,1,0:T(8,128)(2,1)S(1)} %get-tuple-element.12), channel_id=1, replica_groups=mesh['rows'=32,'feat'=4] {'rows'}, dimensions={0} | all-to-all | bytes 786432 | tf_op jit(solution)/shard_map/all_to_all | solution.py:230
  29.5 0.1 collective-permute-start.3
  29.6 0.0 copy-start
  29.6 1.7 %first_half.1.partial = f32[2,64,128]{2,1,0:T(8,128)S(1)} custom-call(bf16[32,48,128]{2,1,0:T(8,128)(2,1)S(1)} %all_to_all.5.recv), custom_call_target="tpu_custom_call" | custom-call | flops 1073741824 | bytes 1048576 | tf_op jit(solution)/shard_map/first_half/pallas_call | solution.py:232
  31.3 0.0 collective-permute-done.3.other
  31.3 0.0 copy-done
  31.3 1.9 %histograms.1 = (f32[2,2,16,256]{3,2,1,0:T(8,128)}, s32[12,128]{1,0:T(8,128)}, f32[12,128]{1,0:T(8,128)}) custom-call(bf16[32,48,128]{2,1,0:T(8,128)(2,1)S(1)} %all_to_all.5.recv, bf16[32,12,128]{2,1,0:T(8,128)(2,1)S(1)} %collective-permute-done.3.other, f32[2,64,128]{2,1,0:T(8,128)S(1)} %first_half.1.partial, s32[12,128]{1,0:T(8,128)S(1)} %get-tuple-element.13.code, ...), custom_call_target="tpu_custom_call" | custom-call | tf_op jit(solution)/shard_map/histograms/pallas_call | solution.py:242
  (2 shorter events, 0.1 us)
Async XLA Ops:
  1.8 7.5 %copy-start.2 = (bf16[1536]{0:T(1024)(128)(2,1)S(1)}, bf16[1536]{0:T(1024)(128)(2,1)}, u32[]{:S(2)}) copy-start(bf16[1536]{0:T(1024)(128)(2,1)} %param.10) | copy-start | bytes 9220
  1.9 7.5 %copy-start.1 = (bf16[1536]{0:T(1024)(128)(2,1)S(1)}, bf16[1536]{0:T(1024)(128)(2,1)}, u32[]{:S(2)}) copy-start(bf16[1536]{0:T(1024)(128)(2,1)} %param.9) | copy-start | bytes 9220
  1.9 7.1 %collective-permute-start.2 = (bf16[12,128]{1,0:T(8,128)(2,1)S(1)}, bf16[12,128]{1,0:T(8,128)(2,1)S(1)}, u32[]{:S(2)}, u32[]{:S(2)}) collective-permute-start(bf16[12,128]{1,0:T(8,128)(2,1)S(1)} %get-tuple-element.11.mine), channel_id=1, source_target_pairs={{0,2},{1,3},{2,0},{3,1},{4,6},{5,7},{6,4},{7,5},{8,10},{9,11},{10,... | collective-permute-start | bytes 9224 | tf_op jit(solution)/shard_map/ppermute | solution.py:220
  5.7 3.7 %collective-permute-start.1 = (bf16[12,128]{1,0:T(8,128)(2,1)S(1)}, bf16[12,128]{1,0:T(8,128)(2,1)S(1)}, u32[]{:S(2)}, u32[]{:S(2)}) collective-permute-start(bf16[12,128]{1,0:T(8,128)(2,1)S(1)} %get-tuple-element.11.mine), channel_id=1, source_target_pairs={{0,1},{1,2},{2,3},{3,0},{4,5},{5,6},{6,7},{7,4},{8,9},{9,10},{10,1... | collective-permute-start | bytes 9224 | tf_op jit(solution)/shard_map/ppermute | solution.py:220
  6.1 3.3 %collective-permute-start = (bf16[12,128]{1,0:T(8,128)(2,1)S(1)}, bf16[12,128]{1,0:T(8,128)(2,1)S(1)}, u32[]{:S(2)}, u32[]{:S(2)}) collective-permute-start(bf16[12,128]{1,0:T(8,128)(2,1)S(1)} %get-tuple-element.11.mine), channel_id=1, source_target_pairs={{0,3},{1,0},{2,1},{3,2},{4,7},{5,4},{6,5},{7,6},{8,11},{9,8},{10,9... | collective-permute-start | bytes 9224 | tf_op jit(solution)/shard_map/ppermute | solution.py:220
  29.5 1.8 %collective-permute-start.3 = (bf16[32,12,128]{2,1,0:T(8,128)(2,1)S(1)}, bf16[32,12,128]{2,1,0:T(8,128)(2,1)S(1)}, u32[]{:S(2)}, u32[]{:S(2)}) collective-permute-start(bf16[32,12,128]{2,1,0:T(8,128)(2,1)S(1)} %slice.4), channel_id=1, source_target_pairs={{0,4},{4,0},{8,12},{12,8},{16,20},{20,16},{24,28},{28,24},{32,36},... | collective-permute-start | bytes 294920 | tf_op jit(solution)/shard_map/ppermute | solution.py:231
  29.6 1.7 %copy-start = (f32[1536]{0:T(1024)S(1)}, f32[1536]{0:T(1024)}, u32[]{:S(2)}) copy-start(f32[1536]{0:T(1024)} %param.11) | copy-start | bytes 18436

commit v8 on v7

--- a/solution.py
+++ b/solution.py
@@ -17,7 +17,7 @@
 SMEM = pl.BlockSpec(memory_space=pltpu.SMEM)
 
 
-def split_kernel(bins, leaf, features, cutoffs, part, packed, cells, rows, leaves, wanted, limits, sems):
+def split_kernel(bins, leaf, features, cutoffs, part, rows, cells, leaves, wanted, limits, sems):
     width, length = bins.shape
     blocks = length // LANES
     copies = [(features, wanted), (cutoffs, limits), (leaf, leaves)]
@@ -39,6 +39,10 @@
         child = (2 * slot + (chosen > limits[slot]).astype(jnp.int32)) * here
         code = jnp.where(leaves[...] == slot, child, code)
     part[...] = code.astype(jnp.float32).astype(jnp.bfloat16)
+
+
+def pack_kernel(rows, packed):
+    blocks = packed.shape[1] // 2
     owners, each, _ = packed.shape
     for owner in range(owners):
         core = owner % 2
@@ -201,14 +205,13 @@
     height = 2 * each
     tally = pltpu.VMEM((2 * owners, LANES), jnp.float32)
     columns = pltpu.VMEM((5, owners * blocks * 2 // 3 + GROUP + 16, LANES), jnp.float32)
-    part, packed = pl.pallas_call(
+    part, spread_out = pl.pallas_call(
         split_kernel,
-        out_shape=(shape((blocks, LANES), jnp.bfloat16), shape((owners, each, LANES), jnp.bfloat16)),
+        out_shape=(shape((blocks, LANES), jnp.bfloat16), shape((width * blocks + 8, LANES), jnp.int32)),
         in_specs=[here] * 4,
         out_specs=(VMEM, VMEM),
         scratch_shapes=[
             pltpu.VMEM((width, length), jnp.int32),
-            pltpu.VMEM((width * blocks + 8, LANES), jnp.int32),
             pltpu.VMEM((blocks, LANES), jnp.int32),
             pltpu.SMEM((LEAVES,), jnp.int32),
             pltpu.SMEM((LEAVES,), jnp.int32),
@@ -217,6 +220,14 @@
         name="split_rows",
         compiler_params=SMALL,
     )(*(pltpu.with_memory_space_constraint(x, pltpu.HBM) for x in (bins, tall(leaf), split_feature, split_bin)))
+    packed = pl.pallas_call(
+        pack_kernel,
+        out_shape=shape((owners, each, LANES), jnp.bfloat16),
+        in_specs=[VMEM],
+        out_specs=VMEM,
+        name="pack_bins",
+        compiler_params=SMALL,
+    )(spread_out)
     others = [lax.ppermute(part, "feat", [(i, (i + s) % feats) for i in range(feats)]) for s in (3, 1, 2)]
     send, code = pl.pallas_call(
         fill_kernel,

time: 33.4 us -> 33.2 us (level)
  local copies, waits for them, and re-layouts: 0.03 us -> 0.39 us
    unnamed x6, local copies, waits for them, and re-layouts: 0.02 us -> 0.38 us
    all_to_all x1, blocking collectives: 20.1 us -> 19.8 us  [body(): recv = lax.all_to_all(send, 'rows', 0, 0, tiled=True)]
where the time goes in v8:
time: 33.2 us; the launch traced here: 32.9 us
  blocking collectives  19.8 us (60%)
  starting transfers between devices  6.57 us (20%)
  Pallas kernels  4.64 us (14%)
  between operations  1.37 us (4%)
  local copies, waits for them, and re-layouts  0.39 us (1%)
    all_to_all x1, blocking collectives, body(): recv = lax.all_to_all(send, 'rows', 0, 0, tiled=True)  19.8 us
    ppermute x3, starting transfers between devices, body(): lax.ppermute(part, 'feat', [(i, (i + s) % feats) for i in range(feats)])  6.48 us
    pallas_call x1, Pallas kernels, body(): pl.pallas_call(last_kernel, out_shape=(shape((2, 2, KIDS, B), jnp.float32...  1.71 us
    pallas_call x1, Pallas kernels, body(): pl.pallas_call(first_kernel, out_shape=shape((2, 4 * KIDS, LANES), jnp.fl...  1.67 us
    pallas_call x1, Pallas kernels, body(): pl.pallas_call(split_kernel, out_shape=(shape((blocks, LANES), jnp.bfloat...  1.13 us
  transfers between devices with their start and end apart: 4, of which 1 were waited for; matrix products, arithmetic and copies ran while one was open for 0% of the time, Pallas kernels for 5%

profile of v8, /device:TPU:1, one launch (start us, length us, event | category | flops | bytes accessed | tf_op | source)
XLA Modules:
  0.0 32.9 jit_solution(3838658982147641093)
XLA Ops:
  0.6 1.1 %split_rows.1 = (bf16[12,128]{1,0:T(8,128)(2,1)S(1)}, s32[776,128]{1,0:T(8,128)S(1)}) custom-call(s32[64,1536]{1,0:T(8,128)} %bins.1, s32[12,128]{1,0:T(8,128)} %bitcast.10, s32[8]{0:T(128)} %features.1, s32[8]{0:T(128)} %cutoffs.1), custom_call_target="tpu_custom_call" | custom-call | tf_op jit(solution)/shard_map/split_rows/pallas_call | solution.py:208
  1.8 3.8 %collective-permute-start.2 = (bf16[12,128]{1,0:T(8,128)(2,1)S(1)}, bf16[12,128]{1,0:T(8,128)(2,1)S(1)}, u32[]{:S(2)}, u32[]{:S(2)}) collective-permute-start(bf16[12,128]{1,0:T(8,128)(2,1)S(1)} %get-tuple-element.11.mine), channel_id=1, source_target_pairs={{0,2},{1,3},{2,0},{3,1},{4,6},{5,7},{6,4},{7,5},{8,10},{9,11},{10,... | collective-permute-start | bytes 9224 | tf_op jit(solution)/shard_map/ppermute | solution.py:231
  5.6 0.4 %collective-permute-start.1 = (bf16[12,128]{1,0:T(8,128)(2,1)S(1)}, bf16[12,128]{1,0:T(8,128)(2,1)S(1)}, u32[]{:S(2)}, u32[]{:S(2)}) collective-permute-start(bf16[12,128]{1,0:T(8,128)(2,1)S(1)} %get-tuple-element.11.mine), channel_id=1, source_target_pairs={{0,1},{1,2},{2,3},{3,0},{4,5},{5,6},{6,7},{7,4},{8,9},{9,10},{10,1... | collective-permute-start | bytes 9224 | tf_op jit(solution)/shard_map/ppermute | solution.py:231
  6.0 2.3 %collective-permute-start = (bf16[12,128]{1,0:T(8,128)(2,1)S(1)}, bf16[12,128]{1,0:T(8,128)(2,1)S(1)}, u32[]{:S(2)}, u32[]{:S(2)}) collective-permute-start(bf16[12,128]{1,0:T(8,128)(2,1)S(1)} %get-tuple-element.11.mine), channel_id=1, source_target_pairs={{0,3},{1,0},{2,1},{3,2},{4,7},{5,4},{6,5},{7,6},{8,11},{9,8},{10,9... | collective-permute-start | bytes 9224 | tf_op jit(solution)/shard_map/ppermute | solution.py:231
  8.9 0.0 copy-start.1
  8.9 0.0 copy-start.2
  8.9 0.1 pack_bins.1.packed
  9.0 0.0 collective-permute-done.2.three
  9.0 0.2 collective-permute-done.1.two
  9.2 0.0 collective-permute-done.one
  9.3 0.3 %copy-done.1 = bf16[1536]{0:T(1024)(128)(2,1)S(1)} copy-done((bf16[1536]{0:T(1024)(128)(2,1)S(1)}, bf16[1536]{0:T(1024)(128)(2,1)}, u32[]{:S(2)}) %copy-start.1) | copy-done | bytes 3096
  9.6 0.0 copy-done.2
  9.7 19.8 %all_to_all.5.recv = bf16[32,48,128]{2,1,0:T(8,128)(2,1)S(1)} all-to-all(bf16[32,48,128]{2,1,0:T(8,128)(2,1)S(1)} %get-tuple-element.12), channel_id=1, replica_groups=mesh['rows'=32,'feat'=4] {'rows'}, dimensions={0} | all-to-all | bytes 786432 | tf_op jit(solution)/shard_map/all_to_all | solution.py:241
  29.4 0.1 collective-permute-start.3
  29.5 0.0 copy-start
  29.5 1.7 %first_half.1.partial = f32[2,64,128]{2,1,0:T(8,128)S(1)} custom-call(bf16[32,48,128]{2,1,0:T(8,128)(2,1)S(1)} %all_to_all.5.recv), custom_call_target="tpu_custom_call" | custom-call | flops 1073741824 | bytes 1048576 | tf_op jit(solution)/shard_map/first_half/pallas_call | solution.py:243
  31.2 0.0 collective-permute-done.3.other
  31.2 0.0 copy-done
  31.2 1.7 %histograms.1 = (f32[2,2,16,256]{3,2,1,0:T(8,128)}, s32[12,128]{1,0:T(8,128)}, f32[12,128]{1,0:T(8,128)}) custom-call(bf16[32,48,128]{2,1,0:T(8,128)(2,1)S(1)} %all_to_all.5.recv, bf16[32,12,128]{2,1,0:T(8,128)(2,1)S(1)} %collective-permute-done.3.other, f32[2,64,128]{2,1,0:T(8,128)S(1)} %first_half.1.partial, s32[12,128]{1,0:T(8,128)S(1)} %get-tuple-element.13.code, ...), custom_call_target="tpu_custom_call" | custom-call | tf_op jit(solution)/shard_map/histograms/pallas_call | solution.py:253
  (2 shorter events, 0.1 us)
Async XLA Ops:
  1.8 7.3 %collective-permute-start.2 = (bf16[12,128]{1,0:T(8,128)(2,1)S(1)}, bf16[12,128]{1,0:T(8,128)(2,1)S(1)}, u32[]{:S(2)}, u32[]{:S(2)}) collective-permute-start(bf16[12,128]{1,0:T(8,128)(2,1)S(1)} %get-tuple-element.11.mine), channel_id=1, source_target_pairs={{0,2},{1,3},{2,0},{3,1},{4,6},{5,7},{6,4},{7,5},{8,10},{9,11},{10,... | collective-permute-start | bytes 9224 | tf_op jit(solution)/shard_map/ppermute | solution.py:231
  5.6 3.7 %collective-permute-start.1 = (bf16[12,128]{1,0:T(8,128)(2,1)S(1)}, bf16[12,128]{1,0:T(8,128)(2,1)S(1)}, u32[]{:S(2)}, u32[]{:S(2)}) collective-permute-start(bf16[12,128]{1,0:T(8,128)(2,1)S(1)} %get-tuple-element.11.mine), channel_id=1, source_target_pairs={{0,1},{1,2},{2,3},{3,0},{4,5},{5,6},{6,7},{7,4},{8,9},{9,10},{10,1... | collective-permute-start | bytes 9224 | tf_op jit(solution)/shard_map/ppermute | solution.py:231
  6.0 3.3 %collective-permute-start = (bf16[12,128]{1,0:T(8,128)(2,1)S(1)}, bf16[12,128]{1,0:T(8,128)(2,1)S(1)}, u32[]{:S(2)}, u32[]{:S(2)}) collective-permute-start(bf16[12,128]{1,0:T(8,128)(2,1)S(1)} %get-tuple-element.11.mine), channel_id=1, source_target_pairs={{0,3},{1,0},{2,1},{3,2},{4,7},{5,4},{6,5},{7,6},{8,11},{9,8},{10,9... | collective-permute-start | bytes 9224 | tf_op jit(solution)/shard_map/ppermute | solution.py:231
  8.9 0.7 %copy-start.1 = (bf16[1536]{0:T(1024)(128)(2,1)S(1)}, bf16[1536]{0:T(1024)(128)(2,1)}, u32[]{:S(2)}) copy-start(bf16[1536]{0:T(1024)(128)(2,1)} %param.9) | copy-start | bytes 9220
  8.9 0.7 %copy-start.2 = (bf16[1536]{0:T(1024)(128)(2,1)S(1)}, bf16[1536]{0:T(1024)(128)(2,1)}, u32[]{:S(2)}) copy-start(bf16[1536]{0:T(1024)(128)(2,1)} %param.10) | copy-start | bytes 9220
  29.4 1.8 %collective-permute-start.3 = (bf16[32,12,128]{2,1,0:T(8,128)(2,1)S(1)}, bf16[32,12,128]{2,1,0:T(8,128)(2,1)S(1)}, u32[]{:S(2)}, u32[]{:S(2)}) collective-permute-start(bf16[32,12,128]{2,1,0:T(8,128)(2,1)S(1)} %slice.4), channel_id=1, source_target_pairs={{0,4},{4,0},{8,12},{12,8},{16,20},{20,16},{24,28},{28,24},{32,36},... | collective-permute-start | bytes 294920 | tf_op jit(solution)/shard_map/ppermute | solution.py:242
  29.5 1.7 %copy-start = (f32[1536]{0:T(1024)S(1)}, f32[1536]{0:T(1024)}, u32[]{:S(2)}) copy-start(f32[1536]{0:T(1024)} %param.11) | copy-start | bytes 18436

commit v9 on v6

--- a/solution.py
+++ b/solution.py
@@ -16,7 +16,7 @@
 SMEM = pl.BlockSpec(memory_space=pltpu.SMEM)
 
 
-def split_kernel(bins, leaf, features, cutoffs, part, packed, cells, rows, leaves, wanted, limits, sems):
+def split_kernel(bins, leaf, features, cutoffs, part, rows, cells, leaves, wanted, limits, sems):
     width, length = bins.shape
     blocks = length // LANES
     copies = [(features, wanted), (cutoffs, limits), (leaf, leaves)]
@@ -38,6 +38,10 @@
         child = (2 * slot + (chosen > limits[slot]).astype(jnp.int32)) * here
         code = jnp.where(leaves[...] == slot, child, code)
     part[...] = code.astype(jnp.float32).astype(jnp.bfloat16)
+
+
+def pack_kernel(rows, packed):
+    blocks = packed.shape[1] // 2
     owners, each, _ = packed.shape
     half = blocks // 2
     for owner in range(owners):
@@ -191,14 +195,13 @@
     height = 2 * each
     wide = pltpu.VMEM((owners * height + 8, LANES), jnp.float32)
     columns = pltpu.VMEM((5, owners * blocks // 2 + GROUP + 16, LANES), jnp.float32)
-    part, packed = pl.pallas_call(
+    part, spread_out = pl.pallas_call(
         split_kernel,
-        out_shape=(shape((blocks, LANES), jnp.bfloat16), shape((owners, each, LANES), jnp.bfloat16)),
+        out_shape=(shape((blocks, LANES), jnp.bfloat16), shape((width * blocks + 8, LANES), jnp.int32)),
         in_specs=[here] * 4,
         out_specs=(VMEM, VMEM),
         scratch_shapes=[
             pltpu.VMEM((width, length), jnp.int32),
-            pltpu.VMEM((width * blocks + 8, LANES), jnp.int32),
             pltpu.VMEM((blocks, LANES), jnp.int32),
             pltpu.SMEM((LEAVES,), jnp.int32),
             pltpu.SMEM((LEAVES,), jnp.int32),
@@ -207,6 +210,14 @@
         name="split_rows",
         compiler_params=SMALL,
     )(*(pltpu.with_memory_space_constraint(x, pltpu.HBM) for x in (bins, tall(leaf), split_feature, split_bin)))
+    packed = pl.pallas_call(
+        pack_kernel,
+        out_shape=shape((owners, each, LANES), jnp.bfloat16),
+        in_specs=[VMEM],
+        out_specs=VMEM,
+        name="pack_bins",
+        compiler_params=SMALL,
+    )(spread_out)
     others = [lax.ppermute(part, "feat", [(i, (i + s) % feats) for i in range(feats)]) for s in (2, 1, 3)]
     send, code = pl.pallas_call(
         fill_kernel,

time: 33.3 us -> 33.2 us (level)
  no operation moved by 1% of the time
where the time goes in v9:
time: 33.2 us; the launch traced here: 33 us
  blocking collectives  20.1 us (61%)
  starting transfers between devices  6.57 us (20%)
  Pallas kernels  4.5 us (14%)
  between operations  1.36 us (4%)
  waiting for transfers between devices  0.45 us (1%)
    all_to_all x1, blocking collectives, body(): recv = lax.all_to_all(send, 'rows', 0, 0, tiled=True)  20.1 us
    ppermute x3, starting transfers between devices, body(): lax.ppermute(part, 'feat', [(i, (i + s) % feats) for i in range(feats)])  6.49 us
    pallas_call x1, Pallas kernels, body(): pl.pallas_call(last_kernel, out_shape=(shape((2, 2, KIDS, B), jnp.float32...  2.05 us
    pallas_call x1, Pallas kernels, body(): pl.pallas_call(first_kernel, out_shape=shape((2, 4 * KIDS, LANES), jnp.fl...  1.21 us
    pallas_call x1, Pallas kernels, body(): pl.pallas_call(split_kernel, out_shape=(shape((blocks, LANES), jnp.bfloat...  1.13 us
  transfers between devices with their start and end apart: 4, of which 2 were waited for; matrix products, arithmetic and copies ran while one was open for 0% of the time, Pallas kernels for 4%

profile of v9, /device:TPU:1, one launch (start us, length us, event | category | flops | bytes accessed | tf_op | source)
XLA Modules:
  0.0 33.0 jit_solution(16306391572376703489)
XLA Ops:
  0.6 1.1 %split_rows.1 = (bf16[12,128]{1,0:T(8,128)(2,1)S(1)}, s32[776,128]{1,0:T(8,128)S(1)}) custom-call(s32[64,1536]{1,0:T(8,128)} %bins.1, s32[12,128]{1,0:T(8,128)} %bitcast.10, s32[8]{0:T(128)} %features.1, s32[8]{0:T(128)} %cutoffs.1), custom_call_target="tpu_custom_call" | custom-call | tf_op jit(solution)/shard_map/split_rows/pallas_call | solution.py:198
  1.8 3.8 %collective-permute-start = (bf16[12,128]{1,0:T(8,128)(2,1)S(1)}, bf16[12,128]{1,0:T(8,128)(2,1)S(1)}, u32[]{:S(2)}, u32[]{:S(2)}) collective-permute-start(bf16[12,128]{1,0:T(8,128)(2,1)S(1)} %get-tuple-element.11.mine), channel_id=1, source_target_pairs={{0,2},{1,3},{2,0},{3,1},{4,6},{5,7},{6,4},{7,5},{8,10},{9,11},{10,... | collective-permute-start | bytes 9224 | tf_op jit(solution)/shard_map/ppermute | solution.py:221
  5.6 0.4 %collective-permute-start.1 = (bf16[12,128]{1,0:T(8,128)(2,1)S(1)}, bf16[12,128]{1,0:T(8,128)(2,1)S(1)}, u32[]{:S(2)}, u32[]{:S(2)}) collective-permute-start(bf16[12,128]{1,0:T(8,128)(2,1)S(1)} %get-tuple-element.11.mine), channel_id=1, source_target_pairs={{0,1},{1,2},{2,3},{3,0},{4,5},{5,6},{6,7},{7,4},{8,9},{9,10},{10,1... | collective-permute-start | bytes 9224 | tf_op jit(solution)/shard_map/ppermute | solution.py:221
  6.0 2.3 %collective-permute-start.2 = (bf16[12,128]{1,0:T(8,128)(2,1)S(1)}, bf16[12,128]{1,0:T(8,128)(2,1)S(1)}, u32[]{:S(2)}, u32[]{:S(2)}) collective-permute-start(bf16[12,128]{1,0:T(8,128)(2,1)S(1)} %get-tuple-element.11.mine), channel_id=1, source_target_pairs={{0,3},{1,0},{2,1},{3,2},{4,7},{5,4},{6,5},{7,6},{8,11},{9,8},{10,9... | collective-permute-start | bytes 9224 | tf_op jit(solution)/shard_map/ppermute | solution.py:221
  8.3 0.0 copy-start.2
  8.3 0.1 pack_bins.1.packed
  8.3 0.0 copy-start.1
  9.0 0.0 collective-permute-done.one
  9.0 0.2 collective-permute-done.1.two
  9.3 0.0 collective-permute-done.2.three
  9.3 0.0 copy-done.2
  9.3 0.0 copy-done.1
  9.3 20.1 %all_to_all.5.recv = bf16[32,48,128]{2,1,0:T(8,128)(2,1)S(1)} all-to-all(bf16[32,48,128]{2,1,0:T(8,128)(2,1)S(1)} %get-tuple-element.12), channel_id=1, replica_groups=mesh['rows'=32,'feat'=4] {'rows'}, dimensions={0} | all-to-all | bytes 786432 | tf_op jit(solution)/shard_map/all_to_all | solution.py:231
  29.4 0.1 collective-permute-start.3
  29.5 0.0 copy-start
  29.6 1.2 %first_half.1.partial = f32[2,64,128]{2,1,0:T(8,128)S(1)} custom-call(bf16[32,48,128]{2,1,0:T(8,128)(2,1)S(1)} %all_to_all.5.recv), custom_call_target="tpu_custom_call" | custom-call | flops 1073741824 | bytes 1048576 | tf_op jit(solution)/shard_map/first_half/pallas_call | solution.py:233
  30.8 0.2 collective-permute-done.3.other
  31.0 0.0 copy-done
  31.0 2.1 %histograms.1 = (f32[2,2,16,256]{3,2,1,0:T(8,128)}, s32[12,128]{1,0:T(8,128)}, f32[12,128]{1,0:T(8,128)}) custom-call(bf16[32,48,128]{2,1,0:T(8,128)(2,1)S(1)} %all_to_all.5.recv, bf16[32,24,128]{2,1,0:T(8,128)(2,1)S(1)} %collective-permute-done.3.other, f32[2,64,128]{2,1,0:T(8,128)S(1)} %first_half.1.partial, s32[12,128]{1,0:T(8,128)S(1)} %get-tuple-element.13.code, ...), custom_call_target="tpu_custom_call" | custom-call | tf_op jit(solution)/shard_map/histograms/pallas_call | solution.py:243
  (2 shorter events, 0.1 us)
Async XLA Ops:
  1.8 7.2 %collective-permute-start = (bf16[12,128]{1,0:T(8,128)(2,1)S(1)}, bf16[12,128]{1,0:T(8,128)(2,1)S(1)}, u32[]{:S(2)}, u32[]{:S(2)}) collective-permute-start(bf16[12,128]{1,0:T(8,128)(2,1)S(1)} %get-tuple-element.11.mine), channel_id=1, source_target_pairs={{0,2},{1,3},{2,0},{3,1},{4,6},{5,7},{6,4},{7,5},{8,10},{9,11},{10,... | collective-permute-start | bytes 9224 | tf_op jit(solution)/shard_map/ppermute | solution.py:221
  5.6 3.7 %collective-permute-start.1 = (bf16[12,128]{1,0:T(8,128)(2,1)S(1)}, bf16[12,128]{1,0:T(8,128)(2,1)S(1)}, u32[]{:S(2)}, u32[]{:S(2)}) collective-permute-start(bf16[12,128]{1,0:T(8,128)(2,1)S(1)} %get-tuple-element.11.mine), channel_id=1, source_target_pairs={{0,1},{1,2},{2,3},{3,0},{4,5},{5,6},{6,7},{7,4},{8,9},{9,10},{10,1... | collective-permute-start | bytes 9224 | tf_op jit(solution)/shard_map/ppermute | solution.py:221
  6.0 3.3 %collective-permute-start.2 = (bf16[12,128]{1,0:T(8,128)(2,1)S(1)}, bf16[12,128]{1,0:T(8,128)(2,1)S(1)}, u32[]{:S(2)}, u32[]{:S(2)}) collective-permute-start(bf16[12,128]{1,0:T(8,128)(2,1)S(1)} %get-tuple-element.11.mine), channel_id=1, source_target_pairs={{0,3},{1,0},{2,1},{3,2},{4,7},{5,4},{6,5},{7,6},{8,11},{9,8},{10,9... | collective-permute-start | bytes 9224 | tf_op jit(solution)/shard_map/ppermute | solution.py:221
  8.3 1.0 %copy-start.2 = (bf16[1536]{0:T(1024)(128)(2,1)S(1)}, bf16[1536]{0:T(1024)(128)(2,1)}, u32[]{:S(2)}) copy-start(bf16[1536]{0:T(1024)(128)(2,1)} %param.10) | copy-start | bytes 9220
  8.3 0.9 %copy-start.1 = (bf16[1536]{0:T(1024)(128)(2,1)S(1)}, bf16[1536]{0:T(1024)(128)(2,1)}, u32[]{:S(2)}) copy-start(bf16[1536]{0:T(1024)(128)(2,1)} %param.9) | copy-start | bytes 9220
  29.4 1.5 %collective-permute-start.3 = (bf16[32,24,128]{2,1,0:T(8,128)(2,1)S(1)}, bf16[32,24,128]{2,1,0:T(8,128)(2,1)S(1)}, u32[]{:S(2)}, u32[]{:S(2)}) collective-permute-start(bf16[32,24,128]{2,1,0:T(8,128)(2,1)S(1)} %slice.4), channel_id=1, source_target_pairs={{0,4},{4,0},{8,12},{12,8},{16,20},{20,16},{24,28},{28,24},{32,36},... | collective-permute-start | bytes 589832 | tf_op jit(solution)/shard_map/ppermute | solution.py:232
  29.5 1.4 %copy-start = (f32[1536]{0:T(1024)S(1)}, f32[1536]{0:T(1024)}, u32[]{:S(2)}) copy-start(f32[1536]{0:T(1024)} %param.11) | copy-start | bytes 18436
